TPU v7x, 256 devices: a whole 4x4x8 slice. The times are simulated.
256 devices in a mesh: gx: 16 (over z, y_lo), gy: 16 (over x, y_hi, core).
Axes of the slice: x: 4, y: 4 (y_hi: 2, y_lo: 2; y = y_hi * 2 + y_lo), z: 8, core: 2. Of those that a mesh axis runs over, the one named last changes fastest.
Arguments:
- preserved_vector: float32 [14, 128, 128, 128], P(None, 'gx', 'gy'), may hold values from -200 to 200, as said below
- nasa_table: float32 [32, 6], replicated, may hold values from -4 to 4.5, as said below
- gas_constant: float32 [32], replicated, may hold values from 0.3 to 3
- species_index: int32 [9], replicated, may hold values from 0 to 31, as said below
- face_kind: int32 [16, 16, 2], P('gx', 'gy'), may hold values from 0 to 1
Outputs:
- increment: float32 [14, 128, 128, 128], P(None, 'gx', 'gy')
Inputs may be any that keep to these rules, and one draw needn't show every extreme that they name: `preserved_vector`: every cell is a physical state: positive partial densities and an energy whose temperature lies between 0.5 and 2.5. `nasa_table`: each row's cp over R polynomial exceeds 1.5 for temperatures 0.3 to 3. `species_index`: 9 distinct rows.
All inputs are finite; a program needn't handle non-finite values.
Results may differ from a plain program's by a relative error of at most 0.0003.
Values sent between devices are 32-bit elements; how exact they have to be, the bound alone decides.
A program may use at most 64 MiB of HBM per device.

v0:
```python
import jax
import jax.numpy as jnp
from jax import lax
from jax.sharding import Mesh
from jax.sharding import PartitionSpec as P

NS = 9
NVAR = 14
NEWTON = 2
GX_GY = ("gx_0", "gx_1", "gy_0", "gy_1", "gy_2")
GX = ("gx_0", "gx_1")
GY = ("gy_0", "gy_1", "gy_2")


EPSILON = 1e-06
COURANT = 0.8


def by_axis(shard, axes):
    for axis in axes:
        shard = lax.pmax(shard, axis)
    return shard


def padded_2(shard, sides, width):
    edges = {}
    for axis, dim in sides:
        size, length = (lax.axis_size(axis), shard.shape[dim])
        up = [(i, (i + 1) % size) for i in range(size)]
        last = lax.slice_in_dim(shard, length - width, length, axis=dim)
        leading = lax.slice_in_dim(shard, 0, width, axis=dim)
        edges[dim] = (
            lax.ppermute(last, axis, up),
            lax.ppermute(leading, axis, [(b, a) for a, b in up]),
        )
    done = []
    for _, dim in sides:
        low, high = edges[dim]
        around = [(width, width) if d in done else (0, 0) for d in range(shard.ndim)]
        shard = jnp.concatenate([jnp.pad(low, around), shard, jnp.pad(high, around)], axis=dim)
        done.append(dim)
    return shard


def column(vector, trailing_sizes):
    return vector.reshape((vector.shape[0],) + (1,) * trailing_sizes)


def caloric_fitted_curves_table(nasa_table_weights, kelvin_reading):
    trailing_sizes = kelvin_reading.ndim
    columns = [column(nasa_table_weights[:, degree], trailing_sizes) for degree in range(6)]
    replicated_layer = kelvin_reading[None]
    caloric_quotient = columns[0] + replicated_layer * (
        columns[1]
        + replicated_layer
        * (columns[2] + replicated_layer * (columns[3] + replicated_layer * columns[4]))
    )
    chemical_heat_content = columns[5] + replicated_layer * (
        columns[0]
        + replicated_layer
        * (
            columns[1] / 2.0
            + replicated_layer
            * (
                columns[2] / 3.0
                + replicated_layer * (columns[3] / 4.0 + replicated_layer * columns[4] / 5.0)
            )
        )
    )
    return (caloric_quotient, chemical_heat_content)


def solve_for_kelvin(preserved_vector_lines, nasa_table_weights, component_kind_r_factor):
    prefix_addition_result = preserved_vector_lines[:NS]
    bulk_compactness = jnp.sum(prefix_addition_result, axis=0)
    momentum = preserved_vector_lines[NS : NS + 3]
    caloric_content_inner = (
        preserved_vector_lines[NS + 3]
        - 0.5 * jnp.sum(momentum * momentum, axis=0) / bulk_compactness
    )
    blend_stack_lane = column(component_kind_r_factor, bulk_compactness.ndim)
    kelvin_reading = jnp.ones_like(bulk_compactness)
    for iteration in range(NEWTON):
        caloric_quotient, chemical_heat_content = caloric_fitted_curves_table(
            nasa_table_weights, kelvin_reading
        )
        solver_misfit = (
            jnp.sum(
                prefix_addition_result
                * blend_stack_lane
                * (chemical_heat_content - kelvin_reading[None]),
                axis=0,
            )
            - caloric_content_inner
        )
        tangent_steepness_fn = jnp.sum(
            prefix_addition_result * blend_stack_lane * (caloric_quotient - 1.0), axis=0
        )
        kelvin_reading = kelvin_reading - solver_misfit / tangent_steepness_fn
    return kelvin_reading


def nasa_fitted_monomials(
    preserved_vector_lines, kelvin_reading, nasa_table_weights, component_kind_r_factor
):
    prefix_addition_result = preserved_vector_lines[:NS]
    bulk_compactness = jnp.sum(prefix_addition_result, axis=0)
    momentum = preserved_vector_lines[NS : NS + 3]
    doubled_norm_motion = jnp.sum(momentum * momentum, axis=0) / (
        bulk_compactness * bulk_compactness
    )
    blend_stack_lane = column(component_kind_r_factor, bulk_compactness.ndim)
    caloric_quotient, chemical_heat_content = caloric_fitted_curves_table(
        nasa_table_weights, kelvin_reading
    )
    caloric_tiers = blend_stack_lane * (chemical_heat_content - kelvin_reading[None])
    averaged_mixing_law_r = jnp.sum(prefix_addition_result * blend_stack_lane, axis=0)
    thrust_load_quiet = averaged_mixing_law_r * kelvin_reading
    heat_quotient_decrement = averaged_mixing_law_r / jnp.sum(
        prefix_addition_result * blend_stack_lane * (caloric_quotient - 1.0), axis=0
    )
    sound_speed = jnp.sqrt((1.0 + heat_quotient_decrement) * thrust_load_quiet / bulk_compactness)
    force_spatial_jump = (
        blend_stack_lane * kelvin_reading[None]
        - heat_quotient_decrement[None] * caloric_tiers
        + 0.5 * heat_quotient_decrement[None] * doubled_norm_motion[None]
    )
    return jnp.concatenate(
        [
            thrust_load_quiet[None],
            heat_quotient_decrement[None],
            sound_speed[None],
            force_spatial_jump,
        ],
        axis=0,
    )


def reconstruct(values):
    value_zero, value_one, value_two, value_three, value_four = values
    candidate_zero = (2.0 * value_zero - 7.0 * value_one + 11.0 * value_two) / 6.0
    candidate_one = (-value_one + 5.0 * value_two + 2.0 * value_three) / 6.0
    candidate_two = (2.0 * value_two + 5.0 * value_three - value_four) / 6.0
    curve_zero = value_zero - 2.0 * value_one + value_two
    slope_zero = value_zero - 4.0 * value_one + 3.0 * value_two
    curve_one = value_one - 2.0 * value_two + value_three
    slope_one = value_one - value_three
    curve_two = value_two - 2.0 * value_three + value_four
    slope_two = 3.0 * value_two - 4.0 * value_three + value_four
    smooth_zero = 13.0 / 12.0 * curve_zero * curve_zero + 0.25 * slope_zero * slope_zero
    smooth_one = 13.0 / 12.0 * curve_one * curve_one + 0.25 * slope_one * slope_one
    smooth_two = 13.0 / 12.0 * curve_two * curve_two + 0.25 * slope_two * slope_two
    weight_zero = 0.1 / ((EPSILON + smooth_zero) * (EPSILON + smooth_zero))
    weight_one = 0.6 / ((EPSILON + smooth_one) * (EPSILON + smooth_one))
    weight_two = 0.3 / ((EPSILON + smooth_two) * (EPSILON + smooth_two))
    return (
        weight_zero * candidate_zero + weight_one * candidate_one + weight_two * candidate_two
    ) / (weight_zero + weight_one + weight_two)


def window(array, offset, count, array_axis):
    return lax.slice_in_dim(array, offset, offset + count, axis=array_axis)


def direction_rate(preserved_vector_lines, cell_coef, array_axis, normal, speed):
    cells = preserved_vector_lines.shape[array_axis] - 6
    faces = cells + 1
    bulk_compactness = jnp.sum(preserved_vector_lines[:NS], axis=0)
    fractions = preserved_vector_lines[:NS] / bulk_compactness[None]
    velocity = preserved_vector_lines[NS : NS + 3] / bulk_compactness[None]
    passive = preserved_vector_lines[NS + 4 : NS + 5] / bulk_compactness[None]
    thrust_load_quiet = cell_coef[0]
    normal_speed = velocity[normal]
    carried = preserved_vector_lines * normal_speed[None]
    flux_rows = [carried[:NS]]
    for component in range(3):
        if component == normal:
            flux_rows.append((carried[NS + component] + thrust_load_quiet)[None])
        else:
            flux_rows.append(carried[NS + component][None])
    flux_rows.append((carried[NS + 3] + thrust_load_quiet * normal_speed)[None])
    flux_rows.append(carried[NS + 4][None])
    physical = jnp.concatenate(flux_rows, axis=0)
    upwind = 0.5 * (physical + speed * preserved_vector_lines)
    downwind = 0.5 * (physical - speed * preserved_vector_lines)

    def average(array):
        return 0.5 * (window(array, 2, faces, array_axis) + window(array, 3, faces, array_axis))

    mean_frac = average(fractions)
    mean_vel = average(velocity)
    mean_passive = average(passive)[0]
    mean_gamma = average(cell_coef[1:2])[0]
    mean_sound = average(cell_coef[2:3])[0]
    mean_slopes = average(cell_coef[3:])
    mean_square = jnp.sum(mean_vel * mean_vel, axis=0)
    mean_enthalpy = (
        mean_sound * mean_sound - jnp.sum(mean_frac * mean_slopes, axis=0)
    ) / mean_gamma + mean_square
    inverse = 1.0 / (mean_sound * mean_sound)
    tangents = [component for component in range(3) if component != normal]

    def project(vector):
        total = jnp.sum(vector[:NS], axis=0)
        pressure_jump = (
            jnp.sum(mean_slopes * vector[:NS], axis=0)
            - mean_gamma * jnp.sum(mean_vel * vector[NS : NS + 3], axis=0)
            + mean_gamma * vector[NS + 3]
        )
        normal_jump = vector[NS + normal] - mean_vel[normal] * total
        scaled = pressure_jump * inverse
        slower = 0.5 * (pressure_jump - mean_sound * normal_jump) * inverse
        faster = 0.5 * (pressure_jump + mean_sound * normal_jump) * inverse
        species = vector[:NS] - mean_frac * scaled[None]
        first_shear = vector[NS + tangents[0]] - mean_vel[tangents[0]] * total
        second_shear = vector[NS + tangents[1]] - mean_vel[tangents[1]] * total
        scalar_wave = vector[NS + 4] - mean_passive * scaled
        return jnp.concatenate(
            [
                slower[None],
                species,
                first_shear[None],
                second_shear[None],
                faster[None],
                scalar_wave[None],
            ],
            axis=0,
        )

    rising = reconstruct(
        [project(window(upwind, offset, faces, array_axis)) for offset in (0, 1, 2, 3, 4)]
    )
    falling = reconstruct(
        [project(window(downwind, offset, faces, array_axis)) for offset in (5, 4, 3, 2, 1)]
    )
    amplitude = rising + falling
    slower = amplitude[0]
    species = amplitude[1 : NS + 1]
    first_shear = amplitude[NS + 1]
    second_shear = amplitude[NS + 2]
    faster = amplitude[NS + 3]
    scalar_wave = amplitude[NS + 4]
    species_total = jnp.sum(species, axis=0)
    acoustic = slower + faster
    normal_vel = mean_vel[normal]
    momentum_rows = []
    for component in range(3):
        if component == normal:
            momentum_rows.append(
                (normal_vel - mean_sound) * slower
                + (normal_vel + mean_sound) * faster
                + normal_vel * species_total
            )
        elif component == tangents[0]:
            momentum_rows.append(mean_vel[component] * (acoustic + species_total) + first_shear)
        else:
            momentum_rows.append(mean_vel[component] * (acoustic + species_total) + second_shear)
    energy_row = (
        (mean_enthalpy - normal_vel * mean_sound) * slower
        + (mean_enthalpy + normal_vel * mean_sound) * faster
        + jnp.sum((mean_square[None] - mean_slopes / mean_gamma[None]) * species, axis=0)
        + mean_vel[tangents[0]] * first_shear
        + mean_vel[tangents[1]] * second_shear
    )
    face_flux = jnp.concatenate(
        [
            mean_frac * acoustic[None] + species,
            jnp.stack(momentum_rows, axis=0),
            energy_row[None],
            (mean_passive * acoustic + scalar_wave)[None],
        ],
        axis=0,
    )
    return window(face_flux, 0, cells, array_axis) - window(face_flux, 1, cells, array_axis)


def wall_pad(payload, lower_kind, upper_kind):
    rows_count = payload.shape[0]
    sign_flips = (
        jnp.where(jnp.arange(rows_count) == NS + 2, -1.0, 1.0)
        .astype(payload.dtype)
        .reshape((rows_count, 1, 1, 1))
    )
    lower_copy = jnp.concatenate([payload[..., :1]] * 3, axis=3)
    upper_copy = jnp.concatenate([payload[..., -1:]] * 3, axis=3)
    lower_mirror = payload[..., 2::-1] * sign_flips
    upper_mirror = payload[..., :-4:-1] * sign_flips
    lower_ghost = jnp.where(lower_kind == 1, lower_mirror, lower_copy)
    upper_ghost = jnp.where(upper_kind == 1, upper_mirror, upper_copy)
    return jnp.concatenate([lower_ghost, payload, upper_ghost], axis=3)


def fill_rims(padded):
    preserved_vector_lines = padded[:NVAR]
    return (preserved_vector_lines, padded[NVAR:])


def shards(preserved_vector, nasa_table, gas_constant, species_index, face_kind):
    selector = (
        species_index[:, None] == jnp.arange(nasa_table.shape[0], dtype=jnp.int32)[None, :]
    ).astype(jnp.float32)
    nasa_table_weights = jnp.dot(selector, nasa_table, precision=lax.Precision.HIGHEST)
    component_kind_r_factor = jnp.dot(
        selector, gas_constant[:, None], precision=lax.Precision.HIGHEST
    )[:, 0]
    kelvin_reading = solve_for_kelvin(preserved_vector, nasa_table_weights, component_kind_r_factor)
    self_coefficient = nasa_fitted_monomials(
        preserved_vector, kelvin_reading, nasa_table_weights, component_kind_r_factor
    )
    bulk_compactness = jnp.sum(preserved_vector[:NS], axis=0)
    velocity = preserved_vector[NS : NS + 3] / bulk_compactness[None]
    local_speed = jnp.max(jnp.abs(velocity) + self_coefficient[2][None], axis=(1, 2, 3))
    speeds = by_axis(local_speed, GX_GY)
    joined = jnp.concatenate([preserved_vector, self_coefficient], axis=0)
    padded_both = padded_2(joined, ((GX, 1), (GY, 2)), 3)
    padded_x = padded_both[:, :, 3:-3]
    padded_y = padded_both[:, 3:-3, :]
    padded_z = wall_pad(joined, face_kind[0, 0, 0], face_kind[0, 0, 1])
    rate = direction_rate(padded_z[:NVAR], padded_z[NVAR:], 3, 2, speeds[2])
    state_x, coef_x = fill_rims(padded_x)
    rate = rate + direction_rate(state_x, coef_x, 1, 0, speeds[0])
    state_y, coef_y = fill_rims(padded_y)
    rate = rate + direction_rate(state_y, coef_y, 2, 1, speeds[1])
    return COURANT / jnp.sum(speeds) * rate


def solution(mesh):
    finer = Mesh(mesh.devices.reshape(8, 2, 4, 2, 2), ("gx_0", "gx_1", "gy_0", "gy_1", "gy_2"))
    placed = (P(None, GX, GY, None), P(), P(), P(), P(GX, GY, None))
    return jax.shard_map(
        shards, mesh=finer, in_specs=placed, out_specs=P(None, GX, GY, None), check_vma=False
    )
```

profile of v0, /device:TPU:1, one launch (start us, length us, event | category | flops | bytes accessed | tf_op | source)
XLA Modules:
  0.0 112.2 jit_solution(6320281386992279448)
XLA Ops:
  1.6 0.9 multiply_reduce_fusion.41
  2.5 1.1 constant_dynamic-update-slice_fusion.4
  4.4 1.1 multiply_reduce_fusion.37
  8.1 2.1 %collective-permute-start = (f32[26,3,8,128]{3,2,1,0:T(8,128)}, f32[26,3,8,128]{3,2,1,0:T(8,128)}, u32[]{:S(2)}, u32[]{:S(2)}) collective-permute-start(f32[26,3,8,128]{3,2,1,0:T(8,128)} %get-tuple-element.534), channel_id=1, source_target_pairs={{0,16},{16,32},{32,48},{48,64},{64,80},{80,96},{96,112},{112,128},... | collective-permute-start | bytes 958472 | tf_op jit(solution)/shard_map/ppermute | solution.py:33
  10.2 5.3 %collective-permute-start.1 = (f32[26,3,8,128]{3,2,1,0:T(8,128)}, f32[26,3,8,128]{3,2,1,0:T(8,128)}, u32[]{:S(2)}, u32[]{:S(2)}) collective-permute-start(f32[26,3,8,128]{3,2,1,0:T(8,128)} %get-tuple-element.535), channel_id=1, source_target_pairs={{16,0},{32,16},{48,32},{64,48},{80,64},{96,80},{112,96},{128,112},... | collective-permute-start | bytes 958472 | tf_op jit(solution)/shard_map/ppermute | solution.py:34
  16.5 1.0 collective-permute-start.3
  18.2 2.5 %collective-permute-start.2 = (f32[26,8,3,128]{3,1,2,0:T(8,128)}, f32[26,8,3,128]{3,1,2,0:T(8,128)}, u32[]{:S(2)}, u32[]{:S(2)}) collective-permute-start(f32[26,8,3,128]{3,1,2,0:T(8,128)} %copy.1152), channel_id=1, source_target_pairs={{0,1},{1,2},{2,3},{3,4},{4,5},{5,6},{6,7},{7,8},{8,9},{9,10},{10,1... | collective-permute-start | bytes 958472 | tf_op jit(solution)/shard_map/ppermute | solution.py:33
  20.7 1.2 %fusion.363 = (f32[26,8,8,1]{3,2,1,0:T(8,128)}, f32[26,8,8,1]{3,2,1,0:T(8,128)S(1)}) fusion(f32[26,8,8,128]{3,2,1,0:T(8,128)S(1)} %constant_dynamic-update-slice_fusion), kind=kLoop, calls=%fused_computation.1072 | loop fusion | bytes 26624 | tf_op jit(solution)/shard_map/slice | solution.py:284
  23.2 13.0 %pmax.35 = f32[3]{0:T(128)S(1)} all-reduce(f32[3]{0:T(128)S(1)} %add_reduce_fusion), channel_id=1, replica_groups=mesh['gx_0'=8,'gx_1'=2,'gy_0'=4,'gy_1'=2,'gy_2'=2] {'gx_0'}, use_global_device_ids=true, to_apply=%region_9.0 | all-reduce | flops 3 | bytes 24 | tf_op jit(solution)/shard_map/pmax | solution.py:21
  36.2 4.1 %pmax.36 = f32[3]{0:T(128)S(1)} all-reduce(f32[3]{0:T(128)S(1)} %pmax.35), channel_id=1, replica_groups=mesh['gx_0'=8,'gx_1'=2,'gy_0'=4,'gy_1'=2,'gy_2'=2] {'gx_1'}, use_global_device_ids=true, to_apply=%region_10.0 | all-reduce | flops 3 | bytes 24 | tf_op jit(solution)/shard_map/pmax | solution.py:21
  41.6 8.2 %pmax.37 = f32[3]{0:T(128)S(1)} all-reduce(f32[3]{0:T(128)S(1)} %pmax.36), channel_id=1, replica_groups=mesh['gx_0'=8,'gx_1'=2,'gy_0'=4,'gy_1'=2,'gy_2'=2] {'gy_0'}, use_global_device_ids=true, to_apply=%region_11.0 | all-reduce | flops 3 | bytes 24 | tf_op jit(solution)/shard_map/pmax | solution.py:21
  49.7 2.4 %copy.1156 = f32[26,8,8,1]{2,1,0,3:T(8,128)S(1)} copy(f32[26,8,8,1]{3,2,1,0:T(8,128)} %get-tuple-element.530) | data formatting | bytes 13312 | tf_op jit(solution)/shard_map/slice | solution.py:284
  52.2 1.9 %copy.1157 = f32[26,8,8,1]{2,1,0,3:T(8,128)} copy(f32[26,8,8,1]{3,2,1,0:T(8,128)S(1)} %get-tuple-element.531) | data formatting | bytes 13312 | tf_op jit(solution)/shard_map/slice | solution.py:285
  54.1 1.2 %rev.6 = f32[26,8,8,3]{3,2,1,0:T(8,128)} reverse(f32[26,8,8,3]{3,2,1,0:T(8,128)S(1)} %get-tuple-element.532), dimensions={3} | reverse | bytes 39936 | tf_op jit(solution)/shard_map/rev | solution.py:286
  55.3 1.2 %rev.7 = f32[26,8,8,3]{3,2,1,0:T(8,128)} reverse(f32[26,8,8,3]{3,2,1,0:T(8,128)S(1)} %get-tuple-element.533), dimensions={3} | reverse | bytes 39936 | tf_op jit(solution)/shard_map/rev | solution.py:287
  56.5 2.0 %multiply_select_fusion.1 = (f32[26,8,8,3]{3,2,1,0:T(8,128)S(1)}, f32[26,8,8,3]{3,2,1,0:T(8,128)S(1)}) fusion(f32[26,8,8,3]{3,2,1,0:T(8,128)} %rev.6, f32[26,8,8]{2,1,0:T(8,128)S(1)} %bitcast.929, f32[26]{0:T(128)S(1)} %compare_select_fusion, pred[]{:T(512)} %bitcast.19, f32[26,8,8]{2,1,0:T(8,128)S(1)} %bitcast.930, f32[26,8,8,3]{3,2,1,0:T(8,128)} %rev.7, ...), kind=kLoop, calls=%fused_computation.55 | loop fusion | flops 19968 | bytes 93290 | tf_op jit(solution)/shard_map/jit(_where)/select_n | solution.py:288
  59.3 1.1 %copy-done.2 = f32[26,8,8,134]{3,2,1,0:T(8,128)} copy-done((f32[26,8,8,134]{3,2,1,0:T(8,128)}, f32[26,8,8,134]{3,2,1,0:T(8,128)S(1)}, u32[]{:S(2)}) %copy-start.2) | copy-done | bytes 891928
  60.7 6.4 %pmax.38 = f32[3]{0:T(128)S(1)} all-reduce(f32[3]{0:T(128)S(1)} %pmax.37), channel_id=1, replica_groups=mesh['gx_0'=8,'gx_1'=2,'gy_0'=4,'gy_1'=2,'gy_2'=2] {'gy_1'}, use_global_device_ids=true, to_apply=%region_12.0 | all-reduce | flops 3 | bytes 24 | tf_op jit(solution)/shard_map/pmax | solution.py:21
  67.0 1.2 %slice_multiply_fusion.1 = f32[14,8,8,134]{3,2,1,0:T(8,128)S(1)} fusion(f32[26,8,8,134]{3,2,1,0:T(8,128)} %copy-done.2, f32[8,8,134]{2,1,0:T(8,128)S(1)} %slice_bitcast_fusion), kind=kLoop, calls=%fused_computation.53 | loop fusion | flops 120064 | bytes 994816 | tf_op jit(solution)/shard_map/mul | solution.py:174
  69.2 0.9 slice.1845
  70.2 8.4 %pmax.39 = f32[3]{0:T(128)S(1)} all-reduce(f32[3]{0:T(128)S(1)} %pmax.38), channel_id=1, replica_groups=mesh['gx_0'=8,'gx_1'=2,'gy_0'=4,'gy_1'=2,'gy_2'=2] {'gy_2'}, use_global_device_ids=true, to_apply=%region_13.0 | all-reduce | flops 3 | bytes 24 | tf_op jit(solution)/shard_map/pmax | solution.py:21
  80.2 2.3 %subtract_multiply_fusion = (f32[14,8,8,134]{3,2,1,0:T(8,128)S(1)}, f32[14,8,8,134]{3,2,1,0:T(8,128)S(1)}) fusion(f32[26,8,8,134]{3,2,1,0:T(8,128)} %copy-done.2, f32[1,8,8,134]{3,2,1,0:T(8,128)S(1)} %copy-done.6, f32[1,8,8,134]{3,2,1,0:T(8,128)S(1)} %slice_add_fusion.8, f32[1,8,8,134]{3,2,1,0:T(8,128)S(1)} %get-tuple-element.266, ...), kind=kLoop, calls=%fused_computation.50 | loop fusion | flops 960512 | bytes 1921028 | tf_op jit(solution)/shard_map/mul | solution.py:185
  82.4 0.9 slice_reduce_fusion.11
  84.8 1.4 %subtract_dynamic-update-slice_fusion.8 = (f32[14,8,8,129]{3,2,1,0:T(8,128)S(1)}, f32[14,8,8,129]{3,2,1,0:T(8,128)S(1)}, f32[14,8,8,129]{3,2,1,0:T(8,128)S(1)}, ...) fusion(f32[14,8,8,129]{3,2,1,0:T(8,128)S(1)} %get-tuple-element, ...), kind=kLoop, calls=%fused_computation.112 | loop fusion | flops 1841088 | bytes 9830400
  88.8 4.4 %divide_add_fusion = f32[14,8,8,129]{3,2,1,0:T(8,128)S(1)} fusion(f32[14,8,8,129]{3,2,1,0:T(8,128)S(1)} %get-tuple-element.404, f32[14,8,8,129]{3,2,1,0:T(8,128)S(1)} %get-tuple-element.402, f32[14,8,8,129]{3,2,1,0:T(8,128)S(1)} %get-tuple-element.403, f32[14,8,8,129]{3,2,1,0:T(8,128)S(1)} %get-tuple-element.405, ...), kind=kLoop, calls=%fused_computation.49 | loop fusion | flops 14910336 | bytes 5085696 | tf_op jit(solution)/shard_map/add | solution.py:236
  95.0 1.2 %pad_maximum_fusion.2 = f32[26,14,8,128]{3,2,1,0:T(8,128)S(1)} fusion(f32[26,3,8,128]{3,2,1,0:T(8,128)} %collective-permute-done.1, f32[26,8,8,128]{3,2,1,0:T(8,128)S(1)} %constant_dynamic-update-slice_fusion, f32[26,3,8,128]{3,2,1,0:T(8,128)} %collective-permute-done), kind=kLoop, calls=%fused_computation.10 | loop fusion | flops 745472 | bytes 2981888 | tf_op jit(solution)/shard_map/concatenate | solution.py:40
  96.5 1.0 pad.8
  97.6 1.0 pad.7
  100.2 1.0 slice_reduce_fusion.34
  103.1 2.3 %divide_add_fusion.2 = f32[14,9,8,128]{3,2,1,0:T(8,128)S(1)} fusion(f32[14,9,8,128]{3,2,1,0:T(8,128)S(1)} %get-tuple-element.518, f32[14,9,8,128]{3,2,1,0:T(8,128)S(1)} %get-tuple-element.516, f32[14,9,8,128]{3,2,1,0:T(8,128)S(1)} %get-tuple-element.517, f32[14,9,8,128]{3,2,1,0:T(8,128)S(1)} %get-tuple-element.519, ...), kind=kLoop, calls=%fused_computation.181 | loop fusion | flops 16644096 | bytes 5677056 | tf_op jit(solution)/shard_map/add | solution.py:236
  108.4 2.3 %divide_add_fusion.1 = f32[14,8,9,128]{3,1,2,0:T(8,128)S(1)} fusion(f32[14,8,9,128]{3,1,2,0:T(8,128)S(1)} %get-tuple-element.495, f32[14,8,9,128]{3,1,2,0:T(8,128)S(1)} %get-tuple-element.493, f32[14,8,9,128]{3,1,2,0:T(8,128)S(1)} %get-tuple-element.494, f32[14,8,9,128]{3,1,2,0:T(8,128)S(1)} %get-tuple-element.496, ...), kind=kLoop, calls=%fused_computation.180 | loop fusion | flops 16644096 | bytes 5677056 | tf_op jit(solution)/shard_map/add | solution.py:236
  111.1 1.1 fusion.78
  (155 shorter events, 23.2 us)
Async XLA Ops:
  0.0 0.7 copy-start
  0.0 6.3 %copy-start.3 = (f32[14,8,8,128]{3,2,1,0:T(8,128)S(1)}, f32[14,8,8,128]{3,2,1,0:T(8,128)}, u32[]{:S(2)}) copy-start(f32[14,8,8,128]{3,2,1,0:T(8,128)} %param.5) | copy-start | bytes 1376260
  8.1 86.8 %collective-permute-start = (f32[26,3,8,128]{3,2,1,0:T(8,128)}, f32[26,3,8,128]{3,2,1,0:T(8,128)}, u32[]{:S(2)}, u32[]{:S(2)}) collective-permute-start(f32[26,3,8,128]{3,2,1,0:T(8,128)} %get-tuple-element.534), channel_id=1, source_target_pairs={{0,16},{16,32},{32,48},{48,64},{64,80},{80,96},{96,112},{112,128},... | collective-permute-start | bytes 958472 | tf_op jit(solution)/shard_map/ppermute | solution.py:33
  10.2 84.7 %collective-permute-start.1 = (f32[26,3,8,128]{3,2,1,0:T(8,128)}, f32[26,3,8,128]{3,2,1,0:T(8,128)}, u32[]{:S(2)}, u32[]{:S(2)}) collective-permute-start(f32[26,3,8,128]{3,2,1,0:T(8,128)} %get-tuple-element.535), channel_id=1, source_target_pairs={{16,0},{32,16},{48,32},{64,48},{80,64},{96,80},{112,96},{128,112},... | collective-permute-start | bytes 958472 | tf_op jit(solution)/shard_map/ppermute | solution.py:34
  16.5 80.0 %collective-permute-start.3 = (f32[26,8,3,128]{3,1,2,0:T(8,128)}, f32[26,8,3,128]{3,1,2,0:T(8,128)}, u32[]{:S(2)}, u32[]{:S(2)}) collective-permute-start(f32[26,8,3,128]{3,1,2,0:T(8,128)} %copy.1153), channel_id=1, source_target_pairs={{1,0},{2,1},{3,2},{4,3},{5,4},{6,5},{7,6},{8,7},{9,8},{10,9},{11,1... | collective-permute-start | bytes 958472 | tf_op jit(solution)/shard_map/ppermute | solution.py:34
  18.2 79.4 %collective-permute-start.2 = (f32[26,8,3,128]{3,1,2,0:T(8,128)}, f32[26,8,3,128]{3,1,2,0:T(8,128)}, u32[]{:S(2)}, u32[]{:S(2)}) collective-permute-start(f32[26,8,3,128]{3,1,2,0:T(8,128)} %copy.1152), channel_id=1, source_target_pairs={{0,1},{1,2},{2,3},{3,4},{4,5},{5,6},{6,7},{7,8},{8,9},{9,10},{10,1... | collective-permute-start | bytes 958472 | tf_op jit(solution)/shard_map/ppermute | solution.py:33
  21.9 0.7 copy-start.7
  54.1 2.4 %copy-start.5 = (f32[26,8,8,1]{2,1,0,3:T(8,128)S(1)}, f32[26,8,8,1]{2,1,0,3:T(8,128)}, u32[]{:S(2)}) copy-start(f32[26,8,8,1]{2,1,0,3:T(8,128)} %copy.1157) | copy-start | bytes 19972
  59.3 1.2 %copy-start.2 = (f32[26,8,8,134]{3,2,1,0:T(8,128)}, f32[26,8,8,134]{3,2,1,0:T(8,128)S(1)}, u32[]{:S(2)}) copy-start(f32[26,8,8,134]{3,2,1,0:T(8,128)S(1)} %pad_maximum_fusion.1) | copy-start | bytes 2675716
  68.3 1.0 copy-start.4
  69.2 10.9 %copy-start.6 = (f32[1,8,8,134]{3,2,1,0:T(8,128)S(1)}, f32[1,8,8,134]{3,2,1,0:T(8,128)}, u32[]{:S(2)}) copy-start(f32[1,8,8,134]{3,2,1,0:T(8,128)} %get-tuple-element.440) | copy-start | bytes 102916
  111.0 1.2 %copy-start.1 = (f32[32,6]{0,1:T(8,128)S(1)}, f32[32,6]{0,1:T(8,128)}, u32[]{:S(2)}) copy-start(f32[32,6]{0,1:T(8,128)} %param.6) | copy-start | bytes 2308
where the time goes:
time: 113 us; the launch traced here: 112 us
  blocking collectives  40 us (35%)
  other arithmetic  38 us (34%)
  local copies, waits for them, and re-layouts  18.9 us (17%)
  starting transfers between devices  10.9 us (10%)
  between operations  2.78 us (2%)
  matrix products  1.7 us (2%)
    pmax x5, blocking collectives, by_axis(): shard = lax.pmax(shard, axis)  40 us
    add x3, other arithmetic, direction_rate(): amplitude = rising + falling  9.05 us
    ppermute x2, starting transfers between devices, padded_2(): lax.ppermute(leading, axis, [(b, a) for a, b in up])  6.25 us
    unnamed x57, other arithmetic  5.95 us
    unnamed x23, local copies, waits for them, and re-layouts  4.78 us
    ppermute x2, starting transfers between devices, padded_2(): lax.ppermute(last, axis, up)  4.62 us
    mul x3, other arithmetic, direction_rate(): downwind = 0.5 * (physical - speed * preserved_vector_lines)  3.84 us
    slice x2, local copies, waits for them, and re-layouts, wall_pad(): lower_copy = jnp.concatenate([payload[..., :1]] * 3, axis=3)  3.61 us
  transfers between devices with their start and end apart: 4, of which 0 were waited for; matrix products, arithmetic and copies ran while one was open for 31% of the time, Pallas kernels for 0%

commit v1 on v0

v1 whole, which is shorter than its diff:
```python
import functools

import jax
import jax.numpy as jnp
from jax import lax
from jax.experimental import pallas as pl
from jax.experimental.pallas import tpu as pltpu
from jax.sharding import PartitionSpec as P

NS = 9
NVAR = 14
NEWTON = 2
EPSILON = 1e-06
COURANT = 0.8
KX, KY, KZ = 3, 3, 3

ROWS = 14
FACES = 9
ORDER = (
    tuple(range(9)) + (9, 10, 11, 12, 13),
    tuple(range(9)) + (10, 9, 11, 12, 13),
    tuple(range(9)) + (11, 9, 10, 12, 13),
)
NM = 9
T1, T2, EN, SC = 10, 11, 12, 13
CY, CU, CZ, CG, CC, CPHI, CP, CRHO = 0, 9, 12, 13, 14, 15, 24, 25
NCELL = 26
NFLUX = 15


def fill_table(nasa_ref, gas_ref, index_ref, tab_ref):
    for i in range(NS):
        k = index_ref[i]
        r = gas_ref[k]
        a = [nasa_ref[k, n] for n in range(6)]
        tab_ref[i, 0] = r
        tab_ref[i, 1] = r * (a[0] - 1.0)
        tab_ref[i, 2] = r * a[1]
        tab_ref[i, 3] = r * a[2]
        tab_ref[i, 4] = r * a[3]
        tab_ref[i, 5] = r * a[4]
        tab_ref[i, 6] = r * a[5]
        tab_ref[i, 7] = r * a[1] * 0.5
        tab_ref[i, 8] = r * a[2] * (1.0 / 3.0)
        tab_ref[i, 9] = r * a[3] * 0.25
        tab_ref[i, 10] = r * a[4] * 0.2


def cell_row(u, tab_ref):
    rho = u[0]
    for i in range(1, NS):
        rho = rho + u[i]
    inv = 1.0 / rho
    square = u[NM] * u[NM] + u[T1] * u[T1] + u[T2] * u[T2]
    energy = u[EN] - 0.5 * square * inv
    moment = []
    for n in range(7):
        total = u[0] * tab_ref[0, n]
        for i in range(1, NS):
            total = total + u[i] * tab_ref[i, n]
        moment.append(total)
    gas, k1, k2, k3, k4, k5, k6 = moment
    l2, l3, l4, l5 = k2 * 0.5, k3 * (1.0 / 3.0), k4 * 0.25, k5 * 0.2
    base = k6 - energy
    t = 1.0
    for _ in range(NEWTON):
        f = base + t * (k1 + t * (l2 + t * (l3 + t * (l4 + t * l5))))
        slope = k1 + t * (k2 + t * (k3 + t * (k4 + t * k5)))
        t = t - f / slope
    heat = k1 + t * (k2 + t * (k3 + t * (k4 + t * k5)))
    g = gas / heat
    p = gas * t
    c = jnp.sqrt((1.0 + g) * p * inv)
    half_q = 0.5 * square * inv * inv
    half_g, half_t = 0.5 * g, 0.5 * t
    phi = []
    for i in range(NS):
        e = tab_ref[i, 6] + t * (
            tab_ref[i, 1]
            + t * (tab_ref[i, 7] + t * (tab_ref[i, 8] + t * (tab_ref[i, 9] + t * tab_ref[i, 10])))
        )
        phi.append(tab_ref[i, 0] * half_t - half_g * (e - half_q))
    half_inv = 0.5 * inv
    cell = [u[i] * inv for i in range(NS)]
    cell += [u[k] * half_inv for k in (NM, T1, T2)]
    cell += [u[SC] * inv, half_g, 0.5 * c] + phi + [p, rho]
    speed = [jnp.abs(u[k] * inv) + c for k in (NM, T1, T2)]
    return cell, speed


def flux_rows(u, half_v, p, rho, alpha):
    v = half_v + half_v
    plus, minus = [], []
    for k in range(NVAR):
        if k == EN:
            f = (u[k] + p) * v
        elif k == NM:
            f = u[k] * v + p
        else:
            f = u[k] * v
        a = alpha * u[k]
        plus.append(f + a)
        minus.append(f - a)
    a = alpha * rho
    plus.append(u[NM] + a)
    minus.append(u[NM] - a)
    return plus, minus


def weno(d0, d1, d2, d3):
    eps = 3.0 * EPSILON
    a1, a2 = d1 * d1, d2 * d2
    s0 = d0 * (d0 - 2.75 * d1) + (2.5 * a1 + eps)
    s2 = d3 * (d3 - 2.75 * d2) + (2.5 * a2 + eps)
    s1 = (a1 - 1.25 * (d1 * d2)) + (a2 + eps)
    r0, r1, r2 = 1.0 / s0, 1.0 / s1, 1.0 / s2
    w0, w1, w2 = r0 * r0, r1 * r1, 3.0 * (r2 * r2)
    c0, c1, c2 = d1 - d0, d2 - d1, d3 - d2
    x0 = w0 * (c1 - c0)
    number = (x0 + x0) + w2 * (c2 - c1)
    total = (w0 + w2) + 6.0 * w1
    return ((d1 + d2) + d2) - number / total


def face_row(cell, diff, base):
    low, high = cell
    mean = [low[n] + high[n] for n in range(CP)]
    y = mean[CY : CY + NS]
    vn, v1, v2 = mean[CU : CU + 3]
    z, g, c = mean[CZ], mean[CG], mean[CC]
    phi = mean[CPHI : CPHI + NS]
    half_over_c = 0.5 / c
    half_over_cc = 2.0 * half_over_c * half_over_c

    def split(d):
        dp = phi[0] * d[0]
        for i in range(1, NS):
            dp = dp + phi[i] * d[i]
        work = vn * d[NM] + v1 * d[T1] + v2 * d[T2]
        dp = dp + g * (d[EN] - work)
        total = d[NVAR]
        a = dp * half_over_cc
        b = (d[NM] - vn * total) * half_over_c
        return a, a - b, a + b, d[T1] - v1 * total, d[T2] - v2 * total, d[SC] - z * a

    parts = [split(d) for d in diff]

    def both(values):
        return weno(*values[:4]) - weno(*values[4:])

    slow, fast, shear1, shear2, scalar = [both([p[n] for p in parts]) for n in range(1, 6)]
    species = [both([d[i] - y[i] * p[0] for d, p in zip(diff, parts)]) for i in range(NS)]
    acoustic = slow + fast
    half_acoustic = 0.5 * acoustic
    pull = c * (fast - slow)
    total = species[0]
    for i in range(1, NS):
        total = total + species[i]
    carried = acoustic + total
    weight = c * c - 0.5 * functools.reduce(lambda s, i: s + y[i] * phi[i], range(1, NS), y[0] * phi[0])
    heat = functools.reduce(lambda s, i: s + species[i] * phi[i], range(1, NS), species[0] * phi[0])
    square = vn * vn + v1 * v1 + v2 * v2
    energy = (
        (weight * acoustic - heat) / g
        + square * carried
        + vn * pull
        + v1 * shear1
        + v2 * shear2
    )
    rows = [species[i] + y[i] * half_acoustic for i in range(NS)]
    rows += [vn * carried + pull, v1 * carried + shear1, v2 * carried + shear2, energy]
    rows += [z * half_acoustic + scalar]
    return [6.0 * base[k] + rows[k] for k in range(NVAR)]


def compute_kernel(
    u_ref, xl_ref, xh_ref, yl_ref, yh_ref, alpha_ref, nasa_ref, gas_ref, index_ref, kind_ref, out_ref,
    tab, uq, cq, ps, ms, dp, dm, fx, tmp,
):
    fill_table(nasa_ref, gas_ref, index_ref, tab)
    lane = lax.broadcasted_iota(jnp.int32, (8, 128), 1)
    sub = lax.broadcasted_iota(jnp.int32, (8, 128), 0)
    left = lane < 64

    for k in range(NVAR):
        cx, cy = ORDER[0][k], ORDER[1][k]
        for r in range(8):
            uq[3 + r, k] = u_ref[cx, 8 * r : 8 * r + 8, :]
            uq[ROWS + 3 + r, k] = u_ref[cy, pl.ds(r, 8, stride=8), :]
        for r in range(3):
            uq[r, k] = xl_ref[cx, r]
            uq[11 + r, k] = xh_ref[cx, r]
            uq[ROWS + r, k] = yl_ref[cy, r]
            uq[ROWS + 11 + r, k] = yh_ref[cy, r]
    zb = 2 * ROWS
    for pair in range(NVAR // 2):
        a, b = 2 * pair, 2 * pair + 1
        both = jnp.concatenate([u_ref[a], u_ref[b]], axis=0)
        turned = jnp.transpose(both)
        for t in range(8):
            lo, hi = turned[8 * t : 8 * t + 8], turned[64 + 8 * t : 72 + 8 * t]
            tmp[a, 8 * t : 8 * t + 8, :] = jnp.where(left, lo, pltpu.roll(hi, 64, 1))
            tmp[b, 8 * t : 8 * t + 8, :] = jnp.where(left, pltpu.roll(lo, 64, 1), hi)
    low_kind, high_kind = kind_ref[0, 0, 0], kind_ref[0, 0, 1]
    low_wall, high_wall = (low_kind == 1), (high_kind == 1)
    for k in range(NVAR):
        cz = ORDER[2][k]
        rows = [tmp[cz, pl.ds(l, 8, stride=8), :] for l in range(8)]
        for l in range(8):
            uq[zb + 3 + l, k] = rows[l]
        sign = -1.0 if k == NM else 1.0
        for n in range(3):
            inside = pltpu.roll(rows[7 - n], 1, 0)
            ghost = jnp.where(low_wall, sign * rows[n], rows[0])
            edge = jnp.where(left, ghost, pltpu.roll(inside, 64, 1))
            uq[zb + 2 - n, k] = jnp.where(sub == 0, edge, inside)
            inside = pltpu.roll(rows[n], 7, 0)
            ghost = jnp.where(high_wall, sign * rows[7 - n], rows[7])
            edge = jnp.where(left, pltpu.roll(inside, 64, 1), ghost)
            uq[zb + 11 + n, k] = jnp.where(sub == 7, edge, inside)

    @pl.loop(0, 3 * ROWS)
    def _(r):
        cell, _ = cell_row([uq[r, k] for k in range(NVAR)], tab)
        for n in range(NCELL):
            cq[r, n] = cell[n]

    @pl.loop(0, 3)
    def _(d):
        first = d * ROWS
        alpha = alpha_ref[d]

        @pl.loop(0, ROWS)
        def _(r):
            plus, minus = flux_rows(
                [uq[first + r, k] for k in range(NVAR)],
                cq[first + r, CU], cq[first + r, CP], cq[first + r, CRHO], alpha,
            )
            for k in range(NFLUX):
                ps[r, k] = plus[k]
                ms[r, k] = minus[k]

        @pl.loop(0, ROWS - 1)
        def _(r):
            for k in range(NFLUX):
                dp[r, k] = ps[r + 1, k] - ps[r, k]
                dm[r, k] = ms[r + 1, k] - ms[r, k]

        @pl.loop(0, FACES)
        def _(f):
            diff = [[dp[f + n, k] for k in range(NFLUX)] for n in (0, 1, 2, 3)]
            diff += [[dm[f + n, k] for k in range(NFLUX)] for n in (4, 3, 2, 1)]
            base = [ps[f + 2, k] + ms[f + 3, k] for k in range(NVAR)]
            cell = [[cq[first + f + n, k] for k in range(CP)] for n in (2, 3)]
            flux = face_row(cell, diff, base)
            for k in range(NVAR):
                fx[d * FACES + f, k] = flux[k]

    scale = (COURANT / 12.0) / (alpha_ref[0] + alpha_ref[1] + alpha_ref[2])
    for k in range(NVAR):
        for r in range(8):
            tmp[ORDER[1][k], 8 * r : 8 * r + 8, :] = fx[FACES + r, k] - fx[FACES + r + 1, k]
    for k in range(NVAR):
        for r in range(8):
            rate = (fx[r, k] - fx[r + 1, k]) + tmp[k, pl.ds(r, 8, stride=8), :]
            out_ref[k, 8 * r : 8 * r + 8, :] = rate
    for k in range(NVAR):
        for r in range(8):
            tmp[ORDER[2][k], 8 * r : 8 * r + 8, :] = fx[2 * FACES + r, k] - fx[2 * FACES + r + 1, k]
    for pair in range(NVAR // 2):
        a, b = 2 * pair, 2 * pair + 1
        low, high = [], []
        for t in range(8):
            ra = tmp[a, pl.ds(t, 8, stride=8), :]
            rb = tmp[b, pl.ds(t, 8, stride=8), :]
            low.append(jnp.where(left, ra, pltpu.roll(rb, 64, 1)))
            high.append(jnp.where(left, pltpu.roll(ra, 64, 1), rb))
        back = jnp.transpose(jnp.concatenate(low + high, axis=0))
        out_ref[a] = scale * (out_ref[a] + back[:64])
        out_ref[b] = scale * (out_ref[b] + back[64:])


def compute(u, halos, alpha, nasa, gas, index, kind):
    vmem = pl.BlockSpec(memory_space=pltpu.VMEM)
    smem = pl.BlockSpec(memory_space=pltpu.SMEM)
    f32 = jnp.float32
    return pl.pallas_call(
        compute_kernel,
        out_shape=jax.ShapeDtypeStruct((NVAR, 64, 128), f32),
        in_specs=[vmem] * 5 + [smem] * 5,
        out_specs=vmem,
        scratch_shapes=[
            pltpu.SMEM((NS, 11), f32),
            pltpu.VMEM((3 * ROWS, NVAR, 8, 128), f32),
            pltpu.VMEM((3 * ROWS, NCELL, 8, 128), f32),
            pltpu.VMEM((ROWS, NFLUX, 8, 128), f32),
            pltpu.VMEM((ROWS, NFLUX, 8, 128), f32),
            pltpu.VMEM((ROWS, NFLUX, 8, 128), f32),
            pltpu.VMEM((ROWS, NFLUX, 8, 128), f32),
            pltpu.VMEM((3 * FACES, NVAR, 8, 128), f32),
            pltpu.VMEM((NVAR, 64, 128), f32),
        ],
    )(u, *halos, alpha, nasa, gas, index, kind)


def local_speeds(u, nasa, gas, index):
    def kernel(u_ref, nasa_ref, gas_ref, index_ref, out_ref, tab):
        fill_table(nasa_ref, gas_ref, index_ref, tab)
        best = None
        for r in range(8):
            _, speed = cell_row([u_ref[k, 8 * r : 8 * r + 8, :] for k in range(NVAR)], tab)
            best = speed if best is None else [jnp.maximum(a, b) for a, b in zip(best, speed)]
        for d in range(3):
            out_ref[d] = best[d]

    vmem = pl.BlockSpec(memory_space=pltpu.VMEM)
    smem = pl.BlockSpec(memory_space=pltpu.SMEM)
    best = pl.pallas_call(
        kernel,
        out_shape=jax.ShapeDtypeStruct((3, 8, 128), jnp.float32),
        in_specs=[vmem] + [smem] * 3,
        out_specs=vmem,
        scratch_shapes=[pltpu.SMEM((NS, 11), jnp.float32)],
    )(u, nasa, gas, index)
    return jnp.max(best, axis=(1, 2))


def solution(mesh):
    def shards(u, nasa, gas, index, kind):
        flat = u.reshape(NVAR, 64, 128)
        alpha = lax.pmax(local_speeds(flat, nasa, gas, index), ("gx", "gy"))
        halos = []
        for axis, dim in (("gx", 1), ("gy", 2)):
            n = mesh.shape[axis]
            up = [(i, (i + 1) % n) for i in range(n)]
            for piece, pairs in (
                (lax.slice_in_dim(u, 5, 8, axis=dim), up),
                (lax.slice_in_dim(u, 0, 3, axis=dim), [(b, a) for a, b in up]),
            ):
                if dim == 2:
                    piece = jnp.swapaxes(piece, 1, 2)
                halos.append(lax.ppermute(piece, axis, pairs))
        out = compute(flat, halos, alpha, nasa, gas, index, kind)
        return out.reshape(u.shape)

    whole = P(None, "gx", "gy", None)
    return jax.shard_map(
        shards, mesh=mesh, in_specs=(whole, P(), P(), P(), P("gx", "gy", None)), out_specs=whole, check_vma=False
    )
```

time: 113 us -> 110 us (0.973)
  other arithmetic: 38 us -> 0.81 us
  blocking collectives: 40 us -> 76.4 us
  Pallas kernels: 0 us -> 17.2 us
  local copies, waits for them, and re-layouts: 18.9 us -> 3.91 us
  between operations: 2.78 us -> 0.08 us
  matrix products: 1.7 us -> 0 us
    pmax x5 -> x1, blocking collectives: 40 us -> 76.4 us  [shards(): alpha = lax.pmax(local_speeds(flat, nasa, gas, index), ('gx', 'gy'))]
    pallas_call x0 -> x2, Pallas kernels: none -> 17.2 us  [the longest x1 15.3 us: compute(): pl.pallas_call(compute_kernel, out_shape=jax.ShapeDtypeStruct((NVAR, 64,...]
    add x5 -> x0, other arithmetic: 10.8 us -> none  [the longest x3 9.05 us: direction_rate(): amplitude = rising + falling]
    mul x21 -> x0, other arithmetic: 8.67 us -> none  [the longest x3 3.84 us: direction_rate(): downwind = 0.5 * (physical - speed * preserved_vector_lines)]
    slice x10 -> x2, local copies, waits for them, and re-layouts: 9.26 us -> 1.18 us  [shards(): lax.slice_in_dim(u, 0, 3, axis=dim)]
    reduce_sum x17 -> x0, other arithmetic: 6.82 us -> none  [the longest x3 2.17 us: project(): total = jnp.sum(vector[:NS], axis=0)]
    unnamed x57 -> x0, other arithmetic: 5.95 us -> none
    concatenate x16 -> x0, other arithmetic: 3.15 us -> none  [the longest x2 1.49 us: padded_2(): jnp.concatenate([jnp.pad(low, around), shard, jnp.pad(high, around)], axi...]
  transfers between devices with their start and end apart: 4 -> 4, of which waited for: 0 -> 0; matrix products, arithmetic and copies ran while one was open for 31% -> 1% of each run, Pallas kernels for 0% -> 2%
where the time goes in v1:
time: 110 us
  blocking collectives  76.4 us (69%)
  Pallas kernels  17.2 us (16%)
  starting transfers between devices  11.1 us (10%)
  local copies, waits for them, and re-layouts  3.91 us (4%)
    pmax x1, blocking collectives, shards(): alpha = lax.pmax(local_speeds(flat, nasa, gas, index), ('gx', 'gy'))  76.4 us
    pallas_call x1, Pallas kernels, compute(): pl.pallas_call(compute_kernel, out_shape=jax.ShapeDtypeStruct((NVAR, 64,...  15.3 us
    ppermute x4, starting transfers between devices, shards(): halos.append(lax.ppermute(piece, axis, pairs))  11.1 us
    unnamed x15, local copies, waits for them, and re-layouts  2.73 us
  transfers between devices with their start and end apart: 4, of which 0 were waited for; matrix products, arithmetic and copies ran while one was open for 1% of the time, Pallas kernels for 2%

profile of v1, /device:TPU:1, one launch (start us, length us, event | category | flops | bytes accessed | tf_op | source)
XLA Modules:
  0.0 109.5 jit_solution(12999642439770396669)
XLA Ops:
  0.0 0.0 copy-start
  0.0 1.1 fusion.1
  1.1 7.5 %collective-permute-start.1 = (f32[14,3,8,128]{3,2,1,0:T(8,128)S(1)}, f32[14,3,8,128]{3,2,1,0:T(8,128)S(1)}, u32[]{:S(2)}, u32[]{:S(2)}) collective-permute-start(f32[14,3,8,128]{3,2,1,0:T(8,128)S(1)} %get-tuple-element.7), channel_id=1, source_target_pairs={{16,0},{32,16},{48,32},{64,48},{80,64},{96,80},{112,96},{128,112},... | collective-permute-start | bytes 516104 | tf_op jit(solution)/shard_map/ppermute | solution.py:342
  8.6 0.0 collective-permute-start
  8.6 0.0 copy-done
  8.6 0.1 fusion
  8.7 3.5 %collective-permute-start.2 = (f32[14,3,8,128]{3,2,1,0:T(8,128)S(1)}, f32[14,3,8,128]{3,2,1,0:T(8,128)S(1)}, u32[]{:S(2)}, u32[]{:S(2)}) collective-permute-start(f32[14,3,8,128]{3,2,1,0:T(8,128)S(1)} %bitcast.10), channel_id=1, source_target_pairs={{0,1},{1,2},{2,3},{3,4},{4,5},{5,6},{6,7},{7,8},{8,9},{9,10},{10,1... | collective-permute-start | bytes 516104 | tf_op jit(solution)/shard_map/ppermute | solution.py:342
  12.2 0.0 copy-start.5
  12.3 0.1 collective-permute-start.3
  12.4 0.6 copy-done.5
  12.9 0.7 copy.8.nasa_ref
  13.6 1.9 %shard_map.55 = f32[3,8,128]{2,1,0:T(8,128)} custom-call(f32[14,64,128]{2,1,0:T(8,128)} %bitcast.8, f32[32,6]{1,0:T(8,128)} %copy.8.nasa_ref, f32[32]{0:T(128)} %gas_ref.3, s32[9]{0:T(128)} %index_ref.3), custom_call_target="tpu_custom_call" | custom-call | tf_op jit(solution)/shard_map/pallas_call | solution.py:318
  15.6 0.8 reduce_max.9
  16.4 76.4 %pmax.7.alpha_ref = f32[3]{0:T(128)} all-reduce(f32[3]{0:T(128)S(1)} %reduce_max.9), channel_id=1, replica_groups=mesh['gx'=16,'gy'=16] {'gx','gy'}, use_global_device_ids=true, to_apply=%region_1.0 | all-reduce | flops 3 | bytes 24 | tf_op jit(solution)/shard_map/pmax | solution.py:331
  92.7 0.0 collective-permute-done.1.xh_ref
  92.8 0.0 copy-start.1
  92.8 0.0 collective-permute-done.xl_ref
  92.8 0.0 copy-start.2
  92.8 0.0 collective-permute-done.2.yl_ref
  92.8 0.0 copy-start.3
  92.8 0.0 collective-permute-done.3.yh_ref
  92.8 0.6 copy-done.1
  93.4 0.1 copy-done.2
  93.5 0.1 copy-done.3
  93.6 0.0 copy-start.4
  93.6 0.7 copy-done.4
  94.2 15.3 %shard_map.56 = f32[14,64,128]{2,1,0:T(8,128)} custom-call(f32[14,64,128]{2,1,0:T(8,128)} %bitcast.9, f32[14,3,8,128]{3,2,1,0:T(8,128)} %copy-done.2, f32[14,3,8,128]{3,2,1,0:T(8,128)} %copy-done.1, f32[14,3,8,128]{3,2,1,0:T(8,128)} %copy-done.3, f32[14,3,8,128]{3,2,1,0:T(8,128)} %copy-done.4, f32[3]{0:T(128)} %pmax.7.alpha_ref, f32[32,6]{1,0:T(8,128)} %copy.8.nasa_ref, ...), custom_call_target="tpu_custom_call" | custom-call | tf_op jit(solution)/shard_map/pallas_call | solution.py:287
  (2 shorter events, 0.0 us)
Async XLA Ops:
  0.0 8.6 %copy-start = (f32[14,8,8,128]{3,2,1,0:T(8,128)S(1)}, f32[14,8,8,128]{3,2,1,0:T(8,128)}, u32[]{:S(2)}) copy-start(f32[14,8,8,128]{3,2,1,0:T(8,128)} %param.5) | copy-start | bytes 1376260
  1.1 91.7 %collective-permute-start.1 = (f32[14,3,8,128]{3,2,1,0:T(8,128)S(1)}, f32[14,3,8,128]{3,2,1,0:T(8,128)S(1)}, u32[]{:S(2)}, u32[]{:S(2)}) collective-permute-start(f32[14,3,8,128]{3,2,1,0:T(8,128)S(1)} %get-tuple-element.7), channel_id=1, source_target_pairs={{16,0},{32,16},{48,32},{64,48},{80,64},{96,80},{112,96},{128,112},... | collective-permute-start | bytes 516104 | tf_op jit(solution)/shard_map/ppermute | solution.py:342
  8.6 84.2 %collective-permute-start = (f32[14,3,8,128]{3,2,1,0:T(8,128)S(1)}, f32[14,3,8,128]{3,2,1,0:T(8,128)S(1)}, u32[]{:S(2)}, u32[]{:S(2)}) collective-permute-start(f32[14,3,8,128]{3,2,1,0:T(8,128)S(1)} %get-tuple-element.8), channel_id=1, source_target_pairs={{0,16},{16,32},{32,48},{48,64},{64,80},{80,96},{96,112},{112,128},... | collective-permute-start | bytes 516104 | tf_op jit(solution)/shard_map/ppermute | solution.py:342
  8.7 84.1 %collective-permute-start.2 = (f32[14,3,8,128]{3,2,1,0:T(8,128)S(1)}, f32[14,3,8,128]{3,2,1,0:T(8,128)S(1)}, u32[]{:S(2)}, u32[]{:S(2)}) collective-permute-start(f32[14,3,8,128]{3,2,1,0:T(8,128)S(1)} %bitcast.10), channel_id=1, source_target_pairs={{0,1},{1,2},{2,3},{3,4},{4,5},{5,6},{6,7},{7,8},{8,9},{9,10},{10,1... | collective-permute-start | bytes 516104 | tf_op jit(solution)/shard_map/ppermute | solution.py:342
  12.2 0.7 copy-start.5
  12.3 80.5 %collective-permute-start.3 = (f32[14,3,8,128]{3,2,1,0:T(8,128)S(1)}, f32[14,3,8,128]{3,2,1,0:T(8,128)S(1)}, u32[]{:S(2)}, u32[]{:S(2)}) collective-permute-start(f32[14,3,8,128]{3,2,1,0:T(8,128)S(1)} %bitcast.11), channel_id=1, source_target_pairs={{1,0},{2,1},{3,2},{4,3},{5,4},{6,5},{7,6},{8,7},{9,8},{10,9},{11,1... | collective-permute-start | bytes 516104 | tf_op jit(solution)/shard_map/ppermute | solution.py:342
  92.8 0.7 copy-start.1
  92.8 0.7 copy-start.2
  92.8 0.8 copy-start.3
  93.6 0.7 copy-start.4

commit v2 on v1

--- a/solution.py
+++ b/solution.py
@@ -188,10 +188,10 @@
             uq[3 + r, k] = u_ref[cx, 8 * r : 8 * r + 8, :]
             uq[ROWS + 3 + r, k] = u_ref[cy, pl.ds(r, 8, stride=8), :]
         for r in range(3):
-            uq[r, k] = xl_ref[cx, r]
-            uq[11 + r, k] = xh_ref[cx, r]
-            uq[ROWS + r, k] = yl_ref[cy, r]
-            uq[ROWS + 11 + r, k] = yh_ref[cy, r]
+            uq[r, k] = xl_ref[cx, 8 * r : 8 * r + 8, :]
+            uq[11 + r, k] = xh_ref[cx, 8 * r : 8 * r + 8, :]
+            uq[ROWS + r, k] = yl_ref[r, cy]
+            uq[ROWS + 11 + r, k] = yh_ref[r, cy]
     zb = 2 * ROWS
     for pair in range(NVAR // 2):
         a, b = 2 * pair, 2 * pair + 1
@@ -228,7 +228,7 @@
     @pl.loop(0, 3)
     def _(d):
         first = d * ROWS
-        alpha = alpha_ref[d]
+        alpha = alpha_ref[0, d]
 
         @pl.loop(0, ROWS)
         def _(r):
@@ -256,7 +256,7 @@
             for k in range(NVAR):
                 fx[d * FACES + f, k] = flux[k]
 
-    scale = (COURANT / 12.0) / (alpha_ref[0] + alpha_ref[1] + alpha_ref[2])
+    scale = (COURANT / 12.0) / (alpha_ref[0, 0] + alpha_ref[0, 1] + alpha_ref[0, 2])
     for k in range(NVAR):
         for r in range(8):
             tmp[ORDER[1][k], 8 * r : 8 * r + 8, :] = fx[FACES + r, k] - fx[FACES + r + 1, k]
@@ -303,45 +303,138 @@
     )(u, *halos, alpha, nasa, gas, index, kind)
 
 
-def local_speeds(u, nasa, gas, index):
-    def kernel(u_ref, nasa_ref, gas_ref, index_ref, out_ref, tab):
-        fill_table(nasa_ref, gas_ref, index_ref, tab)
-        best = None
-        for r in range(8):
-            _, speed = cell_row([u_ref[k, 8 * r : 8 * r + 8, :] for k in range(NVAR)], tab)
-            best = speed if best is None else [jnp.maximum(a, b) for a, b in zip(best, speed)]
-        for d in range(3):
-            out_ref[d] = best[d]
-
+MESH = pl.DeviceIdType.MESH
+
+
+def exchange_kernel(
+    u_ref, nasa_ref, gas_ref, index_ref, alpha_ref, xl_ref, xh_ref, yl_ref, yh_ref,
+    tab, uy, mine, slots, halo_send, halo_recv, speed_send, speed_recv,
+):
+    gx, gy = lax.axis_index("gx"), lax.axis_index("gy")
+    nx, ny = lax.axis_size("gx"), lax.axis_size("gy")
+    z, y_low, plane, core = gx // 2, gx % 2, gy // 2, gy % 2
+    me = (y_low * (ny // 2) + plane, z * 2 + core)
+    size = (ny, nx)
+
+    def member(stage, j):
+        if stage == 0:
+            return (2 * z + j // (ny // 2), 2 * (j % (ny // 2)) + core)
+        return (2 * (j // 2) + y_low, 2 * plane + j % 2)
+
+    others = [[(me[s] + n) % size[s] for n in range(1, size[s])] for s in (0, 1)]
+    beside = [
+        ((gx + 1) % nx, gy),
+        ((gx + nx - 1) % nx, gy),
+        (gx, (gy + 1) % ny),
+        (gx, (gy + ny - 1) % ny),
+    ]
+    barrier = pltpu.get_barrier_semaphore()
+    peers = beside + [member(s, j) for s in (0, 1) for j in others[s]]
+    for peer in peers:
+        pl.semaphore_signal(barrier, inc=1, device_id=peer, device_id_type=MESH)
+
+    fill_table(nasa_ref, gas_ref, index_ref, tab)
+    best = None
+    for r in range(8):
+        _, speed = cell_row([u_ref[k, 8 * r : 8 * r + 8, :] for k in range(NVAR)], tab)
+        best = speed if best is None else [jnp.maximum(a, b) for a, b in zip(best, speed)]
+    lane = lax.broadcasted_iota(jnp.int32, (1, 128), 1)
+    row = jnp.zeros((1, 128), jnp.float32)
+    for d in range(3):
+        row = jnp.where(lane == d, jnp.max(best[d], keepdims=True), row)
+    mine[0] = row
+    for k in range(NVAR):
+        for n, r in enumerate((0, 1, 2, 5, 6, 7)):
+            uy[n, k] = u_ref[k, pl.ds(r, 8, stride=8), :]
+
+    pl.semaphore_wait(barrier, len(peers))
+
+    def speed_copy(stage, n, j, slot):
+        return pltpu.make_async_remote_copy(
+            src_ref=mine.at[stage],
+            dst_ref=slots.at[stage, slot],
+            send_sem=speed_send.at[stage, n],
+            recv_sem=speed_recv.at[stage, slot],
+            device_id=member(stage, j),
+            device_id_type=MESH,
+        )
+
+    def gather(stage):
+        for n, j in enumerate(others[stage]):
+            speed_copy(stage, n, j, me[stage]).start()
+
+    def reduce(stage):
+        total = mine[stage]
+        for n, j in enumerate(others[stage]):
+            speed_copy(stage, n, j, j).wait_recv()
+        for n, j in enumerate(others[stage]):
+            total = jnp.maximum(total, slots[stage, j])
+        return total
+
+    gather(0)
+    pieces = (
+        (u_ref.at[:, 40:64, :], xl_ref),
+        (u_ref.at[:, 0:24, :], xh_ref),
+        (uy.at[3:6], yl_ref),
+        (uy.at[0:3], yh_ref),
+    )
+    halos = []
+    for n, (source, target) in enumerate(pieces):
+        copy = pltpu.make_async_remote_copy(
+            src_ref=source,
+            dst_ref=target,
+            send_sem=halo_send.at[n],
+            recv_sem=halo_recv.at[n],
+            device_id=beside[n],
+            device_id_type=MESH,
+        )
+        copy.start()
+        halos.append(copy)
+    mine[1] = reduce(0)
+    gather(1)
+    alpha_ref[...] = reduce(1)
+    for copy in halos:
+        copy.wait()
+    for stage in (0, 1):
+        for n, j in enumerate(others[stage]):
+            speed_copy(stage, n, j, me[stage]).wait_send()
+
+
+def exchange(u, nasa, gas, index):
     vmem = pl.BlockSpec(memory_space=pltpu.VMEM)
     smem = pl.BlockSpec(memory_space=pltpu.SMEM)
-    best = pl.pallas_call(
-        kernel,
-        out_shape=jax.ShapeDtypeStruct((3, 8, 128), jnp.float32),
+    f32 = jnp.float32
+    shape = jax.ShapeDtypeStruct
+    return pl.pallas_call(
+        exchange_kernel,
+        out_shape=[
+            shape((1, 128), f32),
+            shape((NVAR, 24, 128), f32),
+            shape((NVAR, 24, 128), f32),
+            shape((3, NVAR, 8, 128), f32),
+            shape((3, NVAR, 8, 128), f32),
+        ],
         in_specs=[vmem] + [smem] * 3,
-        out_specs=vmem,
-        scratch_shapes=[pltpu.SMEM((NS, 11), jnp.float32)],
+        out_specs=[vmem] * 5,
+        scratch_shapes=[
+            pltpu.SMEM((NS, 11), f32),
+            pltpu.VMEM((6, NVAR, 8, 128), f32),
+            pltpu.VMEM((2, 1, 128), f32),
+            pltpu.VMEM((2, 16, 1, 128), f32),
+            pltpu.SemaphoreType.DMA((4,)),
+            pltpu.SemaphoreType.DMA((4,)),
+            pltpu.SemaphoreType.DMA((2, 16)),
+            pltpu.SemaphoreType.DMA((2, 16)),
+        ],
+        compiler_params=pltpu.CompilerParams(collective_id=0, has_side_effects=True),
     )(u, nasa, gas, index)
-    return jnp.max(best, axis=(1, 2))
 
 
 def solution(mesh):
     def shards(u, nasa, gas, index, kind):
         flat = u.reshape(NVAR, 64, 128)
-        alpha = lax.pmax(local_speeds(flat, nasa, gas, index), ("gx", "gy"))
-        halos = []
-        for axis, dim in (("gx", 1), ("gy", 2)):
-            n = mesh.shape[axis]
-            up = [(i, (i + 1) % n) for i in range(n)]
-            for piece, pairs in (
-                (lax.slice_in_dim(u, 5, 8, axis=dim), up),
-                (lax.slice_in_dim(u, 0, 3, axis=dim), [(b, a) for a, b in up]),
-            ):
-                if dim == 2:
-                    piece = jnp.swapaxes(piece, 1, 2)
-                halos.append(lax.ppermute(piece, axis, pairs))
-        out = compute(flat, halos, alpha, nasa, gas, index, kind)
-        return out.reshape(u.shape)
+        alpha, *halos = exchange(flat, nasa, gas, index)
+        return compute(flat, halos, alpha, nasa, gas, index, kind).reshape(u.shape)
 
     whole = P(None, "gx", "gy", None)
     return jax.shard_map(

time: 110 us -> 43.3 us (0.39)
  blocking collectives: 76.4 us -> 0 us
  Pallas kernels: 17.2 us -> 41.8 us
  starting transfers between devices: 11.1 us -> 0 us
  local copies, waits for them, and re-layouts: 3.91 us -> 1.36 us
    pmax x1 -> x0, blocking collectives: 76.4 us -> none  [shards(): alpha = lax.pmax(local_speeds(flat, nasa, gas, index), ('gx', 'gy'))]
    pallas_call x1, Pallas kernels: 1.95 us -> 26.5 us  [exchange(): pl.pallas_call(exchange_kernel, out_shape=[shape((1, 128), f32), shape((N...]
    ppermute x4 -> x0, starting transfers between devices: 11.1 us -> none  [shards(): halos.append(lax.ppermute(piece, axis, pairs))]
    unnamed x15 -> x1, local copies, waits for them, and re-layouts: 2.73 us -> 1.36 us
    slice x2 -> x0, local copies, waits for them, and re-layouts: 1.18 us -> none  [shards(): lax.slice_in_dim(u, 0, 3, axis=dim)]
  transfers between devices with their start and end apart: 4 -> 0, of which waited for: 0 -> 0; matrix products, arithmetic and copies ran while one was open for 1% -> 0% of each run, Pallas kernels for 2% -> 0%
where the time goes in v2:
time: 43.3 us; the launch traced here: 43.2 us
  Pallas kernels  41.8 us (97%)
  local copies, waits for them, and re-layouts  1.36 us (3%)
    pallas_call x1, Pallas kernels, exchange(): pl.pallas_call(exchange_kernel, out_shape=[shape((1, 128), f32), shape((N...  26.5 us
    pallas_call x1, Pallas kernels, compute(): pl.pallas_call(compute_kernel, out_shape=jax.ShapeDtypeStruct((NVAR, 64,...  15.3 us
    unnamed x1, local copies, waits for them, and re-layouts  1.36 us

profile of v2, /device:TPU:1, one launch (start us, length us, event | category | flops | bytes accessed | tf_op | source)
XLA Modules:
  0.0 43.2 jit_solution(14184657476170396186)
XLA Ops:
  0.0 1.4 %copy.6.nasa_ref = f32[32,6]{1,0:T(8,128)} copy(f32[32,6]{0,1:T(8,128)} %param.6) | data formatting | bytes 1536 | tf_op args[1]
  1.4 26.5 %shard_map.55 = (f32[1,128]{1,0:T(1,128)}, f32[14,24,128]{2,1,0:T(8,128)}, f32[14,24,128]{2,1,0:T(8,128)}, f32[3,14,8,128]{3,2,1,0:T(8,128)}, f32[3,14,8,128]{3,2,1,0:T(8,128)}) custom-call(f32[14,64,128]{2,1,0:T(8,128)} %bitcast.2, f32[32,6]{1,0:T(8,128)} %copy.6.nasa_ref, f32[32]{0:T(128)} %gas_ref.3, s32[9]{0:T(128)} %index_ref.3), custom_call_target="tpu_custom_call" | custom-call | tf_op jit(solution)/shard_map/pallas_call | solution.py:408
  27.9 15.3 %shard_map.56 = f32[14,64,128]{2,1,0:T(8,128)} custom-call(f32[14,64,128]{2,1,0:T(8,128)} %bitcast.3, f32[14,24,128]{2,1,0:T(8,128)} %get-tuple-element.10.xl_ref, f32[14,24,128]{2,1,0:T(8,128)} %get-tuple-element.11.xh_ref, f32[3,14,8,128]{3,2,1,0:T(8,128)} %get-tuple-element.12.yl_ref, f32[3,14,8,128]{3,2,1,0:T(8,128)} %get-tuple-element.13.yh_ref, ...), custom_call_target="tpu_custom_call" | custom-call | tf_op jit(solution)/shard_map/pallas_call | solution.py:287

commit v3 on v1

v3 whole, which is shorter than its diff:
```python
import functools

import jax
import jax.numpy as jnp
from jax import lax
from jax.experimental import pallas as pl
from jax.experimental.pallas import tpu as pltpu
from jax.sharding import PartitionSpec as P

NS = 9
NVAR = 14
NEWTON = 2
EPSILON = 1e-06
COURANT = 0.8

ROWS = 14
FACES = 9
ORDER = (
    tuple(range(9)) + (9, 10, 11, 12, 13),
    tuple(range(9)) + (10, 9, 11, 12, 13),
    tuple(range(9)) + (11, 9, 10, 12, 13),
)
NM = 9
T1, T2, EN, SC = 10, 11, 12, 13
CY, CU, CZ, CG, CC, CPHI, CRHO, CF = 0, 9, 12, 13, 14, 15, 24, 25
NCELL = 39
FINV, FWEIGHT, FSQUARE = 24, 25, 26
NFACE = 27
MESH = pl.DeviceIdType.MESH


def fill_table(nasa_ref, gas_ref, index_ref, tab_ref):
    for i in range(NS):
        k = index_ref[i]
        r = gas_ref[k]
        a = [nasa_ref[n, k] for n in range(6)]
        tab_ref[i, 0] = r
        tab_ref[i, 1] = r * (a[0] - 1.0)
        tab_ref[i, 2] = r * a[1]
        tab_ref[i, 3] = r * a[2]
        tab_ref[i, 4] = r * a[3]
        tab_ref[i, 5] = r * a[4]
        tab_ref[i, 6] = r * a[5]
        tab_ref[i, 7] = r * a[1] * 0.5
        tab_ref[i, 8] = r * a[2] * (1.0 / 3.0)
        tab_ref[i, 9] = r * a[3] * 0.25
        tab_ref[i, 10] = r * a[4] * 0.2


def cell_row(u, tab_ref):
    rho = u[0]
    for i in range(1, NS):
        rho = rho + u[i]
    inv = 1.0 / rho
    square = u[NM] * u[NM] + u[T1] * u[T1] + u[T2] * u[T2]
    energy = u[EN] - 0.5 * square * inv
    moment = []
    for n in range(7):
        total = u[0] * tab_ref[0, n]
        for i in range(1, NS):
            total = total + u[i] * tab_ref[i, n]
        moment.append(total)
    gas, k1, k2, k3, k4, k5, k6 = moment
    l2, l3, l4, l5 = k2 * 0.5, k3 * (1.0 / 3.0), k4 * 0.25, k5 * 0.2
    base = k6 - energy
    t = 1.0
    for _ in range(NEWTON):
        f = base + t * (k1 + t * (l2 + t * (l3 + t * (l4 + t * l5))))
        slope = k1 + t * (k2 + t * (k3 + t * (k4 + t * k5)))
        t = t - f / slope
    heat = k1 + t * (k2 + t * (k3 + t * (k4 + t * k5)))
    g = gas / heat
    p = gas * t
    c = jnp.sqrt((1.0 + g) * p * inv)
    half_q = 0.5 * square * inv * inv
    half_g, half_t = 0.5 * g, 0.5 * t
    phi = []
    for i in range(NS):
        e = tab_ref[i, 6] + t * (
            tab_ref[i, 1]
            + t * (tab_ref[i, 7] + t * (tab_ref[i, 8] + t * (tab_ref[i, 9] + t * tab_ref[i, 10])))
        )
        phi.append(tab_ref[i, 0] * half_t - half_g * (e - half_q))
    half_inv = 0.5 * inv
    cell = [u[i] * inv for i in range(NS)]
    cell += [u[k] * half_inv for k in (NM, T1, T2)]
    cell += [u[SC] * inv, half_g, 0.5 * c] + phi + [rho]
    v = u[NM] * inv
    flux = [u[k] * v for k in range(NVAR)]
    flux[NM] = flux[NM] + p
    flux[EN] = (u[EN] + p) * v
    cell += flux
    speed = [jnp.abs(u[k] * inv) + c for k in (NM, T1, T2)]
    return cell, speed


def correction(d0, d1, d2, d3):
    a1, a2 = d1 * d1, d2 * d2
    eps = 3.0 * EPSILON
    k1, k2 = 0.609375 * a1 + eps, 0.609375 * a2 + eps
    y0, y1, y2 = d0 - 1.375 * d1, d1 - 0.625 * d2, d3 - 1.375 * d2
    r0, r1, r2 = 1.0 / (y0 * y0 + k1), 1.0 / (y1 * y1 + k2), 1.0 / (y2 * y2 + k2)
    w0, w1, w2 = r0 * r0, r1 * r1, 3.0 * (r2 * r2)
    c0, c1, c2 = d1 - d0, d2 - d1, d3 - d2
    x0 = w0 * (c1 - c0)
    number = (x0 + x0) + w2 * (c2 - c1)
    total = (w0 + w2) + 6.0 * w1
    return number / total


def dot(a, b):
    return functools.reduce(lambda s, n: s + a[n] * b[n], range(1, len(a)), a[0] * b[0])


def prepare(first, f, i, uq, cq, lf, lu, bf, bu, mean_ref):
    low, high = first + f + 2, first + f + 3
    mean = [cq[low, n] + cq[high, n] for n in range(CRHO)]
    y = mean[CY : CY + NS]
    vn, v1, v2 = mean[CU : CU + 3]
    z, g, c = mean[CZ], mean[CG], mean[CC]
    phi = mean[CPHI : CPHI + NS]
    for n in range(CRHO):
        mean_ref[i, n] = mean[n]
    mean_ref[i, FINV] = 1.0 / g
    mean_ref[i, FWEIGHT] = c * c - 0.5 * dot(y, phi)
    mean_ref[i, FSQUARE] = vn * vn + v1 * v1 + v2 * v2
    half_over_c = 0.5 / c
    half_over_cc = 2.0 * half_over_c * half_over_c

    def split(d, total):
        work = vn * d[NM] + v1 * d[T1] + v2 * d[T2]
        dp = dot(phi, d[:NS]) + g * (d[EN] - work)
        a = dp * half_over_cc
        b = (d[NM] - vn * total) * half_over_c
        parts = [d[k] - y[k] * a for k in range(NS)]
        return parts + [a - b, d[T1] - v1 * total, d[T2] - v2 * total, a + b, d[SC] - z * a]

    for n in range(5):
        here, there = first + f + n, first + f + n + 1
        du = [uq[there, k] - uq[here, k] for k in range(NVAR)]
        df = [cq[there, CF + k] - cq[here, CF + k] for k in range(NVAR)]
        parts = split(du, cq[there, CRHO] - cq[here, CRHO])
        for k in range(NVAR):
            lu[i, n, k] = parts[k]
        parts = split(df, du[NM])
        for k in range(NVAR):
            lf[i, n, k] = parts[k]
    for k in range(NVAR):
        f0, f1, f2, f3 = [cq[first + f + n, CF + k] for n in (1, 2, 3, 4)]
        bf[i, k] = 6.0 * (f1 + f2) + ((f1 - f0) - (f3 - f2))
    for k in range(NVAR):
        u0, u1, u2, u3 = [uq[first + f + n, k] for n in (1, 2, 3, 4)]
        bu[i, k] = (u3 - u0) - 3.0 * (u2 - u1)


def finish(alpha, i, lf, lu, bf, bu, mean_ref, fx):
    def wave(k):
        l = [lf[i, n, k] for n in range(5)]
        a = [alpha * lu[i, n, k] for n in range(5)]
        plus = correction(*[l[n] + a[n] for n in (0, 1, 2, 3)])
        minus = correction(*[l[n] - a[n] for n in (4, 3, 2, 1)])
        return minus - plus

    species = [wave(k) for k in range(NS)]
    slow, shear1, shear2, fast, scalar = [wave(k) for k in range(NS, NVAR)]
    mean = [mean_ref[i, n] for n in range(NFACE)]
    y, phi = mean[CY : CY + NS], mean[CPHI : CPHI + NS]
    vn, v1, v2 = mean[CU : CU + 3]
    acoustic = slow + fast
    half_acoustic = 0.5 * acoustic
    pull = mean[CC] * (fast - slow)
    carried = functools.reduce(lambda s, n: s + n, species, acoustic)
    energy = (
        (mean[FWEIGHT] * acoustic - dot(species, phi)) * mean[FINV]
        + mean[FSQUARE] * carried
        + vn * pull
        + v1 * shear1
        + v2 * shear2
    )
    rows = [species[k] + y[k] * half_acoustic for k in range(NS)]
    rows += [vn * carried + pull, v1 * carried + shear1, v2 * carried + shear2, energy]
    rows += [mean[CZ] * half_acoustic + scalar]
    for k in range(NVAR):
        fx[i, k] = (bf[i, k] + alpha * bu[i, k]) + rows[k]


def kernel(
    u_ref, nasa_ref, gas_ref, index_ref, kind_ref, out_ref,
    tab, uq, cq, lf, lu, bf, bu, mean_ref, fx, tmp, alphas,
    mine, slots, halo_send, halo_recv, speed_send, speed_recv,
):
    gx, gy = lax.axis_index("gx"), lax.axis_index("gy")
    nx, ny = lax.axis_size("gx"), lax.axis_size("gy")
    z, y_low, plane, core = gx // 2, gx % 2, gy // 2, gy % 2
    me = (y_low * (ny // 2) + plane, z * 2 + core)
    size = (ny, nx)

    def member(stage, j):
        if stage == 0:
            return (2 * z + j // (ny // 2), 2 * (j % (ny // 2)) + core)
        return (2 * (j // 2) + y_low, 2 * plane + j % 2)

    others = [[(me[s] + n) % size[s] for n in range(1, size[s])] for s in (0, 1)]
    beside = [
        ((gx + 1) % nx, gy),
        ((gx + nx - 1) % nx, gy),
        (gx, (gy + 1) % ny),
        (gx, (gy + ny - 1) % ny),
    ]
    barrier = pltpu.get_barrier_semaphore()
    peers = beside + [member(s, j) for s in (0, 1) for j in others[s]]
    for peer in peers:
        pl.semaphore_signal(barrier, inc=1, device_id=peer, device_id_type=MESH)

    fill_table(nasa_ref, gas_ref, index_ref, tab)
    lane = lax.broadcasted_iota(jnp.int32, (8, 128), 1)
    sub = lax.broadcasted_iota(jnp.int32, (8, 128), 0)
    left = lane < 64
    yb, zb = ROWS, 2 * ROWS

    for k in range(NVAR):
        cx, cy = ORDER[0][k], ORDER[1][k]
        for r in range(8):
            uq[3 + r, k] = u_ref[cx, 8 * r : 8 * r + 8, :]
            uq[yb + 3 + r, k] = u_ref[cy, pl.ds(r, 8, stride=8), :]

    def cells(r):
        cell, speed = cell_row([uq[r, k] for k in range(NVAR)], tab)
        for n in range(NCELL):
            cq[r, n] = cell[n]
        return speed

    zero = jnp.zeros((8, 128), jnp.float32)
    best = lax.fori_loop(
        3, 11, lambda r, best: tuple(jnp.maximum(a, b) for a, b in zip(best, cells(r))), (zero, zero, zero)
    )
    row = jnp.zeros((1, 128), jnp.float32)
    for d in range(3):
        row = jnp.where(lane[:1] == d, jnp.max(best[d], keepdims=True), row)
    mine[0] = row

    pl.semaphore_wait(barrier, len(peers))

    def speed_copy(stage, n, j, slot):
        return pltpu.make_async_remote_copy(
            src_ref=mine.at[stage],
            dst_ref=slots.at[stage, slot],
            send_sem=speed_send.at[stage, n],
            recv_sem=speed_recv.at[stage, slot],
            device_id=member(stage, j),
            device_id_type=MESH,
        )

    def gather(stage):
        for n, j in enumerate(others[stage]):
            speed_copy(stage, n, j, me[stage]).start()

    def reduce(stage):
        total = mine[stage]
        for n, j in enumerate(others[stage]):
            speed_copy(stage, n, j, j).wait_recv()
        for n, j in enumerate(others[stage]):
            total = jnp.maximum(total, slots[stage, j])
        return total

    gather(0)
    pieces = ((8, 0), (3, 11), (yb + 8, yb), (yb + 3, yb + 11))
    halos = [
        pltpu.make_async_remote_copy(
            src_ref=uq.at[source : source + 3],
            dst_ref=uq.at[target : target + 3],
            send_sem=halo_send.at[n],
            recv_sem=halo_recv.at[n],
            device_id=beside[n],
            device_id_type=MESH,
        )
        for n, (source, target) in enumerate(pieces)
    ]
    for copy in halos:
        copy.start()

    for pair in range(NVAR // 2):
        a, b = 2 * pair, 2 * pair + 1
        turned = jnp.transpose(jnp.concatenate([u_ref[a], u_ref[b]], axis=0))
        for t in range(8):
            lo, hi = turned[8 * t : 8 * t + 8], turned[64 + 8 * t : 72 + 8 * t]
            tmp[a, 8 * t : 8 * t + 8, :] = jnp.where(left, lo, pltpu.roll(hi, 64, 1))
            tmp[b, 8 * t : 8 * t + 8, :] = jnp.where(left, pltpu.roll(lo, 64, 1), hi)
    low_wall, high_wall = kind_ref[0, 0, 0] == 1, kind_ref[0, 0, 1] == 1
    for k in range(NVAR):
        cz = ORDER[2][k]
        rows = [tmp[cz, pl.ds(l, 8, stride=8), :] for l in range(8)]
        for l in range(8):
            uq[zb + 3 + l, k] = rows[l]
        sign = -1.0 if k == NM else 1.0
        for n in range(3):
            inside = pltpu.roll(rows[7 - n], 1, 0)
            ghost = jnp.where(low_wall, sign * rows[n], rows[0])
            edge = jnp.where(left, ghost, pltpu.roll(inside, 64, 1))
            uq[zb + 2 - n, k] = jnp.where(sub == 0, edge, inside)
            inside = pltpu.roll(rows[n], 7, 0)
            ghost = jnp.where(high_wall, sign * rows[7 - n], rows[7])
            edge = jnp.where(left, pltpu.roll(inside, 64, 1), ghost)
            uq[zb + 11 + n, k] = jnp.where(sub == 7, edge, inside)

    def before(first, f, i):
        prepare(first, f, i, uq, cq, lf, lu, bf, bu, mean_ref)

    @pl.loop(zb, zb + ROWS)
    def _(r):
        cells(r)

    @pl.loop(yb + 3, yb + 11)
    def _(r):
        cells(r)

    @pl.loop(0, FACES)
    def _(f):
        before(zb, f, 2 * FACES + f)

    @pl.loop(3, 6)
    def _(f):
        before(yb, f, FACES + f)

    mine[1] = reduce(0)
    gather(1)

    halos[0].wait_recv()
    halos[1].wait_recv()

    @pl.loop(0, 6)
    def _(n):
        cells(n + 8 * (n // 3))

    @pl.loop(0, FACES)
    def _(f):
        before(0, f, f)

    speeds = reduce(1)
    total = None
    for d in range(3):
        alpha = jnp.max(jnp.where(lane[:1] == d, speeds, 0.0), keepdims=True)
        alphas[d] = jnp.broadcast_to(alpha, (8, 128))
        total = alphas[d] if total is None else total + alphas[d]
    scale = (COURANT / 12.0) / total

    def after(d, i):
        finish(alphas[d], i, lf, lu, bf, bu, mean_ref, fx)

    @pl.loop(0, 2 * FACES)
    def _(n):
        half = n // FACES
        after(2 * half, n + FACES * half)

    halos[2].wait_recv()
    halos[3].wait_recv()

    @pl.loop(0, 6)
    def _(n):
        cells(yb + n + 8 * (n // 3))

    @pl.loop(0, 6)
    def _(n):
        f = n + 3 * (n // 3)
        before(yb, f, FACES + f)

    @pl.loop(FACES, 2 * FACES)
    def _(i):
        after(1, i)

    for k in range(NVAR):
        for r in range(8):
            tmp[ORDER[1][k], 8 * r : 8 * r + 8, :] = fx[FACES + r, k] - fx[FACES + r + 1, k]
    for k in range(NVAR):
        for r in range(8):
            rate = (fx[r, k] - fx[r + 1, k]) + tmp[k, pl.ds(r, 8, stride=8), :]
            out_ref[k, 8 * r : 8 * r + 8, :] = rate
    for k in range(NVAR):
        for r in range(8):
            tmp[ORDER[2][k], 8 * r : 8 * r + 8, :] = fx[2 * FACES + r, k] - fx[2 * FACES + r + 1, k]
    for pair in range(NVAR // 2):
        a, b = 2 * pair, 2 * pair + 1
        low, high = [], []
        for t in range(8):
            ra = tmp[a, pl.ds(t, 8, stride=8), :]
            rb = tmp[b, pl.ds(t, 8, stride=8), :]
            low.append(jnp.where(left, ra, pltpu.roll(rb, 64, 1)))
            high.append(jnp.where(left, pltpu.roll(ra, 64, 1), rb))
        back = jnp.transpose(jnp.concatenate(low + high, axis=0))
        for r in range(8):
            here = slice(8 * r, 8 * r + 8)
            out_ref[a, here] = scale * (out_ref[a, here] + back[8 * r : 8 * r + 8])
            out_ref[b, here] = scale * (out_ref[b, here] + back[64 + 8 * r : 72 + 8 * r])

    for copy in halos:
        copy.wait_send()
    for stage in (0, 1):
        for n, j in enumerate(others[stage]):
            speed_copy(stage, n, j, me[stage]).wait_send()


def solution(mesh):
    def shards(u, nasa, gas, index, kind):
        vmem = pl.BlockSpec(memory_space=pltpu.VMEM)
        smem = pl.BlockSpec(memory_space=pltpu.SMEM)
        f32 = jnp.float32

        def rows(*lead):
            return pltpu.VMEM(lead + (8, 128), f32)

        out = pl.pallas_call(
            kernel,
            out_shape=jax.ShapeDtypeStruct((NVAR, 64, 128), f32),
            in_specs=[vmem] + [smem] * 4,
            out_specs=vmem,
            scratch_shapes=[
                pltpu.SMEM((NS, 11), f32),
                rows(3 * ROWS, NVAR),
                rows(3 * ROWS, NCELL),
                rows(3 * FACES, 5, NVAR),
                rows(3 * FACES, 5, NVAR),
                rows(3 * FACES, NVAR),
                rows(3 * FACES, NVAR),
                rows(3 * FACES, NFACE),
                rows(3 * FACES, NVAR),
                pltpu.VMEM((NVAR, 64, 128), f32),
                rows(3),
                pltpu.VMEM((2, 1, 128), f32),
                pltpu.VMEM((2, 16, 1, 128), f32),
                pltpu.SemaphoreType.DMA((4,)),
                pltpu.SemaphoreType.DMA((4,)),
                pltpu.SemaphoreType.DMA((2, 16)),
                pltpu.SemaphoreType.DMA((2, 16)),
            ],
            compiler_params=pltpu.CompilerParams(
                collective_id=0, has_side_effects=True, vmem_limit_bytes=56 * 1024 * 1024
            ),
        )(u.reshape(NVAR, 64, 128), nasa.T, gas, index, kind)
        return out.reshape(u.shape)

    whole = P(None, "gx", "gy", None)
    return jax.shard_map(
        shards, mesh=mesh, in_specs=(whole, P(), P(), P(), P("gx", "gy", None)), out_specs=whole, check_vma=False
    )
```

time: 110 us -> 35.7 us (0.32)
  blocking collectives: 76.4 us -> 0 us
  Pallas kernels: 17.2 us -> 33.7 us
  starting transfers between devices: 11.1 us -> 0 us
  local copies, waits for them, and re-layouts: 3.91 us -> 1.82 us
    pmax x1 -> x0, blocking collectives: 76.4 us -> none  [shards(): alpha = lax.pmax(local_speeds(flat, nasa, gas, index), ('gx', 'gy'))]
    pallas_call x2 -> x1, Pallas kernels: 17.2 us -> 33.7 us  [shards(): pl.pallas_call(kernel, out_shape=jax.ShapeDtypeStruct((NVAR, 64, 128), f3...]
    ppermute x4 -> x0, starting transfers between devices: 11.1 us -> none  [shards(): halos.append(lax.ppermute(piece, axis, pairs))]
    slice x2 -> x0, local copies, waits for them, and re-layouts: 1.18 us -> none  [shards(): lax.slice_in_dim(u, 0, 3, axis=dim)]
    unnamed x15 -> x1, local copies, waits for them, and re-layouts: 2.73 us -> 1.82 us
  transfers between devices with their start and end apart: 4 -> 0, of which waited for: 0 -> 0; matrix products, arithmetic and copies ran while one was open for 1% -> 0% of each run, Pallas kernels for 2% -> 0%
where the time goes in v3:
time: 35.7 us; the launch traced here: 35.6 us
  Pallas kernels  33.7 us (94%)
  local copies, waits for them, and re-layouts  1.82 us (5%)
    pallas_call x1, Pallas kernels, shards(): pl.pallas_call(kernel, out_shape=jax.ShapeDtypeStruct((NVAR, 64, 128), f3...  33.7 us
    unnamed x1, local copies, waits for them, and re-layouts  1.82 us

profile of v3, /device:TPU:1, one launch (start us, length us, event | category | flops | bytes accessed | tf_op | source)
XLA Modules:
  0.0 35.6 jit_solution(9776355336144375585)
XLA Ops:
  0.0 33.7 %shard_map.55 = f32[14,64,128]{2,1,0:T(8,128)} custom-call(f32[14,64,128]{2,1,0:T(8,128)} %bitcast.4, f32[6,32]{1,0:T(8,128)} %bitcast.5, f32[32]{0:T(128)} %gas_ref.1, s32[9]{0:T(128)} %index_ref.1, s32[1,1,2]{2,1,0:T(1,128)} %kind_ref.1), custom_call_target="tpu_custom_call" | custom-call | tf_op jit(solution)/shard_map/pallas_call | solution.py:411
  33.8 1.8 %copy.7 = f32[14,8,8,128]{3,2,1,0:T(8,128)} copy(f32[14,8,8,128]{3,2,1,0:T(8,128)} %bitcast.3) | data formatting | bytes 917504

commit v4 on v3

--- a/solution.py
+++ b/solution.py
@@ -147,7 +147,7 @@
             lf[i, n, k] = parts[k]
     for k in range(NVAR):
         f0, f1, f2, f3 = [cq[first + f + n, CF + k] for n in (1, 2, 3, 4)]
-        bf[i, k] = 6.0 * (f1 + f2) + ((f1 - f0) - (f3 - f2))
+        bf[i, k] = 7.0 * (f1 + f2) - (f0 + f3)
     for k in range(NVAR):
         u0, u1, u2, u3 = [uq[first + f + n, k] for n in (1, 2, 3, 4)]
         bu[i, k] = (u3 - u0) - 3.0 * (u2 - u1)
@@ -185,30 +185,44 @@
 
 
 def kernel(
-    u_ref, nasa_ref, gas_ref, index_ref, kind_ref, out_ref,
-    tab, uq, cq, lf, lu, bf, bu, mean_ref, fx, tmp, alphas,
+    u_hbm, nasa_ref, gas_ref, index_ref, kind_ref, out_ref,
+    u_ref, u_sem, tab, uq, cq, lf, lu, bf, bu, mean_ref, fx, tmp, alphas,
     mine, slots, halo_send, halo_recv, speed_send, speed_recv,
 ):
     gx, gy = lax.axis_index("gx"), lax.axis_index("gy")
     nx, ny = lax.axis_size("gx"), lax.axis_size("gy")
     z, y_low, plane, core = gx // 2, gx % 2, gy // 2, gy % 2
-    me = (y_low * (ny // 2) + plane, z * 2 + core)
-    size = (ny, nx)
-
-    def member(stage, j):
+    nz, n_plane = nx // 2, ny // 2
+    x, y_high = plane // 2, plane % 2
+    steps = (
+        sorted(
+            ((dx, high, low) for dx in range(n_plane // 2) for high in (0, 1) for low in (0, 1)),
+            key=lambda d: -min(d[0], n_plane // 2 - d[0]) - (0, 1, 2, 1)[2 * d[1] + d[2]],
+        )[:-1],
+        sorted(((dz, other) for dz in range(nz) for other in (0, 1)), key=lambda d: -min(d[0], nz - d[0]) - 0.1 * d[1])[:-1],
+    )
+
+    def member(stage, step, sign):
         if stage == 0:
-            return (2 * z + j // (ny // 2), 2 * (j % (ny // 2)) + core)
-        return (2 * (j // 2) + y_low, 2 * plane + j % 2)
-
-    others = [[(me[s] + n) % size[s] for n in range(1, size[s])] for s in (0, 1)]
+            dx, high, low = step
+            to_low, to_high = (y_low + low) % 2, (y_high + high) % 2
+            to_x = (x + sign * dx + n_plane // 2) % (n_plane // 2)
+            return (2 * z + to_low, 4 * to_x + 2 * to_high + core), 4 * to_x + 2 * to_high + to_low
+        dz, other = step
+        to_z, to_core = (z + sign * dz + nz) % nz, (core + other) % 2
+        return (2 * to_z + y_low, 2 * plane + to_core), 2 * to_z + to_core
+
+    me = (4 * x + 2 * y_high + y_low, 2 * z + core)
     beside = [
-        ((gx + 1) % nx, gy),
-        ((gx + nx - 1) % nx, gy),
+        ((gx + nx - 1 + 2 * y_low) % nx, gy),
+        (gx + 1 - 2 * y_low, gy),
         (gx, (gy + 1) % ny),
         (gx, (gy + ny - 1) % ny),
     ]
+    load = pltpu.make_async_copy(u_hbm, u_ref, u_sem)
+    load.start()
     barrier = pltpu.get_barrier_semaphore()
-    peers = beside + [member(s, j) for s in (0, 1) for j in others[s]]
+    peers = [member(s, step, 1)[0] for s in (0, 1) for step in steps[s]] + beside
     for peer in peers:
         pl.semaphore_signal(barrier, inc=1, device_id=peer, device_id_type=MESH)
 
@@ -218,11 +232,10 @@
     left = lane < 64
     yb, zb = ROWS, 2 * ROWS
 
-    for k in range(NVAR):
-        cx, cy = ORDER[0][k], ORDER[1][k]
-        for r in range(8):
-            uq[3 + r, k] = u_ref[cx, 8 * r : 8 * r + 8, :]
-            uq[yb + 3 + r, k] = u_ref[cy, pl.ds(r, 8, stride=8), :]
+    load.wait()
+    for k in range(NVAR):
+        for r in range(8):
+            uq[3 + r, k] = u_ref[ORDER[0][k], 8 * r : 8 * r + 8, :]
 
     def cells(r):
         cell, speed = cell_row([uq[r, k] for k in range(NVAR)], tab)
@@ -238,46 +251,6 @@
     for d in range(3):
         row = jnp.where(lane[:1] == d, jnp.max(best[d], keepdims=True), row)
     mine[0] = row
-
-    pl.semaphore_wait(barrier, len(peers))
-
-    def speed_copy(stage, n, j, slot):
-        return pltpu.make_async_remote_copy(
-            src_ref=mine.at[stage],
-            dst_ref=slots.at[stage, slot],
-            send_sem=speed_send.at[stage, n],
-            recv_sem=speed_recv.at[stage, slot],
-            device_id=member(stage, j),
-            device_id_type=MESH,
-        )
-
-    def gather(stage):
-        for n, j in enumerate(others[stage]):
-            speed_copy(stage, n, j, me[stage]).start()
-
-    def reduce(stage):
-        total = mine[stage]
-        for n, j in enumerate(others[stage]):
-            speed_copy(stage, n, j, j).wait_recv()
-        for n, j in enumerate(others[stage]):
-            total = jnp.maximum(total, slots[stage, j])
-        return total
-
-    gather(0)
-    pieces = ((8, 0), (3, 11), (yb + 8, yb), (yb + 3, yb + 11))
-    halos = [
-        pltpu.make_async_remote_copy(
-            src_ref=uq.at[source : source + 3],
-            dst_ref=uq.at[target : target + 3],
-            send_sem=halo_send.at[n],
-            recv_sem=halo_recv.at[n],
-            device_id=beside[n],
-            device_id_type=MESH,
-        )
-        for n, (source, target) in enumerate(pieces)
-    ]
-    for copy in halos:
-        copy.start()
 
     for pair in range(NVAR // 2):
         a, b = 2 * pair, 2 * pair + 1
@@ -303,6 +276,55 @@
             edge = jnp.where(left, pltpu.roll(inside, 64, 1), ghost)
             uq[zb + 11 + n, k] = jnp.where(sub == 7, edge, inside)
 
+    for k in range(NVAR):
+        for r in range(8):
+            uq[yb + 3 + r, k] = u_ref[ORDER[1][k], pl.ds(r, 8, stride=8), :]
+
+    pl.semaphore_wait(barrier, len(peers))
+
+    def speed_copy(stage, n, slot):
+        return pltpu.make_async_remote_copy(
+            src_ref=mine.at[stage],
+            dst_ref=slots.at[stage, slot],
+            send_sem=speed_send.at[stage, n],
+            recv_sem=speed_recv.at[stage, slot],
+            device_id=member(stage, steps[stage][n], 1)[0],
+            device_id_type=MESH,
+        )
+
+    def gather(stage):
+        for n in range(len(steps[stage])):
+            speed_copy(stage, n, me[stage]).start()
+
+    def reduce(stage):
+        total = mine[stage]
+        places = [member(stage, step, -1)[1] for step in steps[stage]]
+        for n, slot in enumerate(places):
+            speed_copy(stage, n, slot).wait_recv()
+        for slot in places:
+            total = jnp.maximum(total, slots[stage, slot])
+        return total
+
+    gather(0)
+    pieces = (
+        (3 + 5 * y_low, 11 - 11 * y_low),
+        (8 - 5 * y_low, 11 * y_low),
+        (yb + 8, yb),
+        (yb + 3, yb + 11),
+    )
+    halos = [
+        pltpu.make_async_remote_copy(
+            src_ref=uq.at[pl.ds(source, 3)],
+            dst_ref=uq.at[pl.ds(target, 3)],
+            send_sem=halo_send.at[n],
+            recv_sem=halo_recv.at[n],
+            device_id=beside[n],
+            device_id_type=MESH,
+        )
+        for n, (source, target) in enumerate(pieces)
+    ]
+    halos[0].start()
+
     def before(first, f, i):
         prepare(first, f, i, uq, cq, lf, lu, bf, bu, mean_ref)
 
@@ -314,27 +336,21 @@
     def _(r):
         cells(r)
 
+    halos[1].start()
     @pl.loop(0, FACES)
     def _(f):
         before(zb, f, 2 * FACES + f)
 
-    @pl.loop(3, 6)
-    def _(f):
-        before(yb, f, FACES + f)
-
     mine[1] = reduce(0)
     gather(1)
-
-    halos[0].wait_recv()
-    halos[1].wait_recv()
-
-    @pl.loop(0, 6)
-    def _(n):
-        cells(n + 8 * (n // 3))
-
-    @pl.loop(0, FACES)
-    def _(f):
-        before(0, f, f)
+    halos[2].start()
+    halos[3].start()
+
+    @pl.loop(0, 6)
+    def _(n):
+        d = n // 3
+        f = 3 + n - 3 * d
+        before(ROWS * d, f, FACES * d + f)
 
     speeds = reduce(1)
     total = None
@@ -347,10 +363,28 @@
     def after(d, i):
         finish(alphas[d], i, lf, lu, bf, bu, mean_ref, fx)
 
-    @pl.loop(0, 2 * FACES)
+    @pl.loop(0, FACES + 6)
     def _(n):
         half = n // FACES
-        after(2 * half, n + FACES * half)
+        m = n - FACES * half
+        d = 2 * (1 - half) + half * (m // 3)
+        after(d, FACES * d + (1 - half) * m + half * (3 + m - 3 * (m // 3)))
+
+    halos[0].wait_recv()
+    halos[1].wait_recv()
+
+    @pl.loop(0, 6)
+    def _(n):
+        cells(n + 8 * (n // 3))
+
+    @pl.loop(0, 6)
+    def _(n):
+        f = n + 3 * (n // 3)
+        before(0, f, f)
+
+    @pl.loop(0, 6)
+    def _(n):
+        after(0, n + 3 * (n // 3))
 
     halos[2].wait_recv()
     halos[3].wait_recv()
@@ -364,9 +398,9 @@
         f = n + 3 * (n // 3)
         before(yb, f, FACES + f)
 
-    @pl.loop(FACES, 2 * FACES)
-    def _(i):
-        after(1, i)
+    @pl.loop(0, 6)
+    def _(n):
+        after(1, FACES + n + 3 * (n // 3))
 
     for k in range(NVAR):
         for r in range(8):
@@ -395,8 +429,8 @@
     for copy in halos:
         copy.wait_send()
     for stage in (0, 1):
-        for n, j in enumerate(others[stage]):
-            speed_copy(stage, n, j, me[stage]).wait_send()
+        for n in range(len(steps[stage])):
+            speed_copy(stage, n, me[stage]).wait_send()
 
 
 def solution(mesh):
@@ -411,9 +445,11 @@
         out = pl.pallas_call(
             kernel,
             out_shape=jax.ShapeDtypeStruct((NVAR, 64, 128), f32),
-            in_specs=[vmem] + [smem] * 4,
+            in_specs=[pl.BlockSpec(memory_space=pl.ANY)] + [smem] * 4,
             out_specs=vmem,
             scratch_shapes=[
+                pltpu.VMEM((NVAR, 64, 128), f32),
+                pltpu.SemaphoreType.DMA,
                 pltpu.SMEM((NS, 11), f32),
                 rows(3 * ROWS, NVAR),
                 rows(3 * ROWS, NCELL),
@@ -433,9 +469,9 @@
                 pltpu.SemaphoreType.DMA((2, 16)),
             ],
             compiler_params=pltpu.CompilerParams(
-                collective_id=0, has_side_effects=True, vmem_limit_bytes=56 * 1024 * 1024
+                collective_id=0, has_side_effects=True, vmem_limit_bytes=36 * 1024 * 1024
             ),
-        )(u.reshape(NVAR, 64, 128), nasa.T, gas, index, kind)
+        )(*[pltpu.with_memory_space_constraint(a, pltpu.HBM) for a in (u.reshape(NVAR, 64, 128), nasa.T, gas, index, kind)])
         return out.reshape(u.shape)
 
     whole = P(None, "gx", "gy", None)

time: 35.7 us -> 31.3 us (0.88)
  Pallas kernels: 33.7 us -> 30.3 us
  local copies, waits for them, and re-layouts: 1.82 us -> 0.77 us
    pallas_call x1, Pallas kernels: 33.7 us -> 30.3 us  [shards(): pl.pallas_call(kernel, out_shape=jax.ShapeDtypeStruct((NVAR, 64, 128), f3...]
    unnamed x1, local copies, waits for them, and re-layouts: 1.82 us -> 0.77 us
where the time goes in v4:
time: 31.3 us; the launch traced here: 31.1 us
  Pallas kernels  30.3 us (97%)
  local copies, waits for them, and re-layouts  0.77 us (2%)
    pallas_call x1, Pallas kernels, shards(): pl.pallas_call(kernel, out_shape=jax.ShapeDtypeStruct((NVAR, 64, 128), f3...  30.3 us
    unnamed x1, local copies, waits for them, and re-layouts  0.77 us

profile of v4, /device:TPU:1, one launch (start us, length us, event | category | flops | bytes accessed | tf_op | source)
XLA Modules:
  0.0 31.1 jit_solution(16965335789464605892)
XLA Ops:
  0.0 30.3 %shard_map.55 = f32[14,64,128]{2,1,0:T(8,128)S(1)} custom-call(f32[14,64,128]{2,1,0:T(8,128)} %bitcast.4, f32[6,32]{1,0:T(8,128)} %bitcast.5, f32[32]{0:T(128)} %gas_ref.1, s32[9]{0:T(128)} %index_ref.1, s32[1,1,2]{2,1,0:T(1,128)} %kind_ref.1), custom_call_target="tpu_custom_call" | custom-call | tf_op jit(solution)/shard_map/pallas_call | solution.py:445
  30.3 0.8 %copy.7 = f32[14,8,8,128]{3,2,1,0:T(8,128)} copy(f32[14,8,8,128]{3,2,1,0:T(8,128)S(1)} %bitcast.3) | data formatting | bytes 917504

commit v5 on v4

--- a/solution.py
+++ b/solution.py
@@ -95,13 +95,13 @@
 
 
 def correction(d0, d1, d2, d3):
-    a1, a2 = d1 * d1, d2 * d2
     eps = 3.0 * EPSILON
-    k1, k2 = 0.609375 * a1 + eps, 0.609375 * a2 + eps
-    y0, y1, y2 = d0 - 1.375 * d1, d1 - 0.625 * d2, d3 - 1.375 * d2
+    c0, c1, c2 = d1 - d0, d2 - d1, d3 - d2
+    m1, m2 = 0.375 * d1, 0.375 * d2
+    k1, k2 = (13.0 / 3.0) * (m1 * m1) + eps, (13.0 / 3.0) * (m2 * m2) + eps
+    y0, y1, y2 = c0 + m1, c1 - m2, c2 - m2
     r0, r1, r2 = 1.0 / (y0 * y0 + k1), 1.0 / (y1 * y1 + k2), 1.0 / (y2 * y2 + k2)
     w0, w1, w2 = r0 * r0, r1 * r1, 3.0 * (r2 * r2)
-    c0, c1, c2 = d1 - d0, d2 - d1, d3 - d2
     x0 = w0 * (c1 - c0)
     number = (x0 + x0) + w2 * (c2 - c1)
     total = (w0 + w2) + 6.0 * w1
@@ -112,18 +112,19 @@
     return functools.reduce(lambda s, n: s + a[n] * b[n], range(1, len(a)), a[0] * b[0])
 
 
-def prepare(first, f, i, uq, cq, lf, lu, bf, bu, mean_ref):
+def face_means(first, f, cq):
     low, high = first + f + 2, first + f + 3
     mean = [cq[low, n] + cq[high, n] for n in range(CRHO)]
-    y = mean[CY : CY + NS]
+    y, phi = mean[CY : CY + NS], mean[CPHI : CPHI + NS]
+    vn, v1, v2 = mean[CU : CU + 3]
+    g, c = mean[CG], mean[CC]
+    return mean + [1.0 / g, c * c - 0.5 * dot(y, phi), vn * vn + v1 * v1 + v2 * v2]
+
+
+def splitter(mean):
+    y, phi = mean[CY : CY + NS], mean[CPHI : CPHI + NS]
     vn, v1, v2 = mean[CU : CU + 3]
     z, g, c = mean[CZ], mean[CG], mean[CC]
-    phi = mean[CPHI : CPHI + NS]
-    for n in range(CRHO):
-        mean_ref[i, n] = mean[n]
-    mean_ref[i, FINV] = 1.0 / g
-    mean_ref[i, FWEIGHT] = c * c - 0.5 * dot(y, phi)
-    mean_ref[i, FSQUARE] = vn * vn + v1 * v1 + v2 * v2
     half_over_c = 0.5 / c
     half_over_cc = 2.0 * half_over_c * half_over_c
 
@@ -135,35 +136,12 @@
         parts = [d[k] - y[k] * a for k in range(NS)]
         return parts + [a - b, d[T1] - v1 * total, d[T2] - v2 * total, a + b, d[SC] - z * a]
 
-    for n in range(5):
-        here, there = first + f + n, first + f + n + 1
-        du = [uq[there, k] - uq[here, k] for k in range(NVAR)]
-        df = [cq[there, CF + k] - cq[here, CF + k] for k in range(NVAR)]
-        parts = split(du, cq[there, CRHO] - cq[here, CRHO])
-        for k in range(NVAR):
-            lu[i, n, k] = parts[k]
-        parts = split(df, du[NM])
-        for k in range(NVAR):
-            lf[i, n, k] = parts[k]
-    for k in range(NVAR):
-        f0, f1, f2, f3 = [cq[first + f + n, CF + k] for n in (1, 2, 3, 4)]
-        bf[i, k] = 7.0 * (f1 + f2) - (f0 + f3)
-    for k in range(NVAR):
-        u0, u1, u2, u3 = [uq[first + f + n, k] for n in (1, 2, 3, 4)]
-        bu[i, k] = (u3 - u0) - 3.0 * (u2 - u1)
-
-
-def finish(alpha, i, lf, lu, bf, bu, mean_ref, fx):
-    def wave(k):
-        l = [lf[i, n, k] for n in range(5)]
-        a = [alpha * lu[i, n, k] for n in range(5)]
-        plus = correction(*[l[n] + a[n] for n in (0, 1, 2, 3)])
-        minus = correction(*[l[n] - a[n] for n in (4, 3, 2, 1)])
-        return minus - plus
-
+    return split
+
+
+def assemble(wave, mean):
     species = [wave(k) for k in range(NS)]
     slow, shear1, shear2, fast, scalar = [wave(k) for k in range(NS, NVAR)]
-    mean = [mean_ref[i, n] for n in range(NFACE)]
     y, phi = mean[CY : CY + NS], mean[CPHI : CPHI + NS]
     vn, v1, v2 = mean[CU : CU + 3]
     acoustic = slow + fast
@@ -179,9 +157,76 @@
     )
     rows = [species[k] + y[k] * half_acoustic for k in range(NS)]
     rows += [vn * carried + pull, v1 * carried + shear1, v2 * carried + shear2, energy]
-    rows += [mean[CZ] * half_acoustic + scalar]
+    return rows + [mean[CZ] * half_acoustic + scalar]
+
+
+def prepare(first, f, i, uq, cq, lf, lu, bf, bu, mean_ref):
+    mean = face_means(first, f, cq)
+    for n in range(NFACE):
+        mean_ref[i, n] = mean[n]
+    split = splitter(mean)
+    for n in range(5):
+        here, there = first + f + n, first + f + n + 1
+        du = [uq[there, k] - uq[here, k] for k in range(NVAR)]
+        df = [cq[there, CF + k] - cq[here, CF + k] for k in range(NVAR)]
+        parts = split(du, cq[there, CRHO] - cq[here, CRHO])
+        for k in range(NVAR):
+            lu[i, n, k] = parts[k]
+        parts = split(df, du[NM])
+        for k in range(NVAR):
+            lf[i, n, k] = parts[k]
+    for k in range(NVAR):
+        f0, f1, f2, f3 = [cq[first + f + n, CF + k] for n in (1, 2, 3, 4)]
+        bf[i, k] = 7.0 * (f1 + f2) - (f0 + f3)
+    for k in range(NVAR):
+        u0, u1, u2, u3 = [uq[first + f + n, k] for n in (1, 2, 3, 4)]
+        bu[i, k] = (u3 - u0) - 3.0 * (u2 - u1)
+
+
+def finish(alpha, i, lf, lu, bf, bu, mean_ref, fx):
+    def wave(k):
+        l = [lf[i, n, k] for n in range(5)]
+        a = [alpha * lu[i, n, k] for n in range(5)]
+        plus = correction(*[l[n] + a[n] for n in (0, 1, 2, 3)])
+        minus = correction(*[l[n] - a[n] for n in (4, 3, 2, 1)])
+        return minus - plus
+
+    rows = assemble(wave, [mean_ref[i, n] for n in range(NFACE)])
     for k in range(NVAR):
         fx[i, k] = (bf[i, k] + alpha * bu[i, k]) + rows[k]
+
+
+def direct(alpha, first, f, i, uq, cq, fx):
+    mean = face_means(first, f, cq)
+    split = splitter(mean)
+    row = first + f
+    plus, minus = [[] for _ in range(4)], [[] for _ in range(4)]
+    for k in range(NVAR + 1):
+        if k < NVAR:
+            l = [cq[row + n, CF + k] for n in range(6)]
+            a = [alpha * uq[row + n, k] for n in range(6)]
+        else:
+            l = [uq[row + n, NM] for n in range(6)]
+            a = [alpha * cq[row + n, CRHO] for n in range(6)]
+        p = [l[n] + a[n] for n in range(5)]
+        m = [l[n] - a[n] for n in range(1, 6)]
+        dp = [p[n + 1] - p[n] for n in range(4)]
+        dm = [m[n + 1] - m[n] for n in range(4)]
+        for n in range(4):
+            plus[n].append(dp[n])
+            minus[n].append(dm[n])
+        if k < NVAR:
+            x = dp[2] - dm[1]
+            fx[i, k] = 6.0 * (p[2] + m[2]) + ((dp[1] - dm[2]) + (x + x))
+    plus = [split(d[:NVAR], d[NVAR]) for d in plus]
+    minus = [split(d[:NVAR], d[NVAR]) for d in minus]
+
+    def wave(k):
+        return correction(*[minus[n][k] for n in (3, 2, 1, 0)]) - correction(*[plus[n][k] for n in (0, 1, 2, 3)])
+
+    rows = assemble(wave, mean)
+    for k in range(NVAR):
+        fx[i, k] = fx[i, k] + rows[k]
 
 
 def kernel(
@@ -194,25 +239,23 @@
     z, y_low, plane, core = gx // 2, gx % 2, gy // 2, gy % 2
     nz, n_plane = nx // 2, ny // 2
     x, y_high = plane // 2, plane % 2
-    steps = (
-        sorted(
-            ((dx, high, low) for dx in range(n_plane // 2) for high in (0, 1) for low in (0, 1)),
-            key=lambda d: -min(d[0], n_plane // 2 - d[0]) - (0, 1, 2, 1)[2 * d[1] + d[2]],
-        )[:-1],
-        sorted(((dz, other) for dz in range(nz) for other in (0, 1)), key=lambda d: -min(d[0], nz - d[0]) - 0.1 * d[1])[:-1],
-    )
-
-    def member(stage, step, sign):
-        if stage == 0:
-            dx, high, low = step
-            to_low, to_high = (y_low + low) % 2, (y_high + high) % 2
-            to_x = (x + sign * dx + n_plane // 2) % (n_plane // 2)
-            return (2 * z + to_low, 4 * to_x + 2 * to_high + core), 4 * to_x + 2 * to_high + to_low
-        dz, other = step
-        to_z, to_core = (z + sign * dz + nz) % nz, (core + other) % 2
-        return (2 * to_z + y_low, 2 * plane + to_core), 2 * to_z + to_core
-
-    me = (4 * x + 2 * y_high + y_low, 2 * z + core)
+    flat_steps = sorted(
+        ((dx, high, low) for dx in range(n_plane // 2) for high in (0, 1) for low in (0, 1)),
+        key=lambda d: -min(d[0], n_plane // 2 - d[0]) - (0, 1, 2, 1)[2 * d[1] + d[2]],
+    )[:-1]
+    tall_steps = sorted(range(1, nz), key=lambda d: -min(d, nz - d))
+
+    def flat(step, sign, to_core):
+        dx, high, low = step
+        to_low, to_high = (y_low + low) % 2, (y_high + high) % 2
+        to_x = (x + sign * dx + n_plane // 2) % (n_plane // 2)
+        return (2 * z + to_low, 4 * to_x + 2 * to_high + to_core), 4 * to_x + 2 * to_high + to_low
+
+    def tall(step, sign, to_core):
+        to_z = (z + sign * step + nz) % nz
+        return (2 * to_z + y_low, 2 * plane + to_core), to_z
+
+    chip = 4 * x + 2 * y_high + y_low
     beside = [
         ((gx + nx - 1 + 2 * y_low) % nx, gy),
         (gx + 1 - 2 * y_low, gy),
@@ -222,9 +265,25 @@
     load = pltpu.make_async_copy(u_hbm, u_ref, u_sem)
     load.start()
     barrier = pltpu.get_barrier_semaphore()
-    peers = [member(s, step, 1)[0] for s in (0, 1) for step in steps[s]] + beside
-    for peer in peers:
+
+    def greet(peer):
         pl.semaphore_signal(barrier, inc=1, device_id=peer, device_id_type=MESH)
+
+    @pl.when(core == 1)
+    def _():
+        for step in flat_steps:
+            greet(flat(step, -1, 0)[0])
+            greet(flat(step, -1, 1)[0])
+        greet((gx, gy - 1))
+
+    for step in tall_steps:
+        greet(tall(step, -1, 1)[0])
+    for peer in beside:
+        greet(peer)
+
+    @pl.when(core == 0)
+    def _():
+        greet((gx, gy + 1))
 
     fill_table(nasa_ref, gas_ref, index_ref, tab)
     lane = lax.broadcasted_iota(jnp.int32, (8, 128), 1)
@@ -280,32 +339,47 @@
         for r in range(8):
             uq[yb + 3 + r, k] = u_ref[ORDER[1][k], pl.ds(r, 8, stride=8), :]
 
-    pl.semaphore_wait(barrier, len(peers))
-
-    def speed_copy(stage, n, slot):
+    to_core_1 = len(flat_steps) + 2 * len(tall_steps) + 1 + len(beside)
+    to_core_0 = len(flat_steps) + 1 + len(beside)
+
+    @pl.when(core == 1)
+    def _():
+        pl.semaphore_wait(barrier, to_core_1)
+
+    @pl.when(core == 0)
+    def _():
+        pl.semaphore_wait(barrier, to_core_0)
+
+
+    def speed_copy(stage, n, slot, peer):
         return pltpu.make_async_remote_copy(
             src_ref=mine.at[stage],
             dst_ref=slots.at[stage, slot],
             send_sem=speed_send.at[stage, n],
             recv_sem=speed_recv.at[stage, slot],
-            device_id=member(stage, steps[stage][n], 1)[0],
+            device_id=peer,
             device_id_type=MESH,
         )
 
-    def gather(stage):
-        for n in range(len(steps[stage])):
-            speed_copy(stage, n, me[stage]).start()
-
-    def reduce(stage):
-        total = mine[stage]
-        places = [member(stage, step, -1)[1] for step in steps[stage]]
-        for n, slot in enumerate(places):
-            speed_copy(stage, n, slot).wait_recv()
-        for slot in places:
-            total = jnp.maximum(total, slots[stage, slot])
-        return total
-
-    gather(0)
+    partner = (gx, gy + 1 - 2 * core)
+    last = len(flat_steps)
+    first_copies = [
+        speed_copy(0, n, 2 * chip + core, flat(step, 1, 1)[0]) for n, step in enumerate(flat_steps)
+    ]
+    second_copies = [
+        speed_copy(1, 2 * n + to_core, z, tall(step, 1, to_core)[0])
+        for n, step in enumerate(tall_steps)
+        for to_core in (0, 1)
+    ] + [speed_copy(1, last, z, partner)]
+    inward = speed_copy(0, last, 2 * chip + core, partner)
+
+    for copy in first_copies:
+        copy.start()
+
+    @pl.when(core == 0)
+    def _():
+        inward.start()
+
     pieces = (
         (3 + 5 * y_low, 11 - 11 * y_low),
         (8 - 5 * y_low, 11 * y_low),
@@ -341,8 +415,19 @@
     def _(f):
         before(zb, f, 2 * FACES + f)
 
-    mine[1] = reduce(0)
-    gather(1)
+    @pl.when(core == 1)
+    def _():
+        places = [2 * flat(step, -1, 1)[1] + side for step in flat_steps for side in (0, 1)] + [2 * chip]
+        for slot in places:
+            speed_copy(0, 0, slot, partner).wait_recv()
+        total = mine[0]
+        for slot in places:
+            total = jnp.maximum(total, slots[0, slot])
+        mine[1] = total
+        for copy in second_copies:
+            copy.start()
+        slots[1, z] = total
+
     halos[2].start()
     halos[3].start()
 
@@ -352,7 +437,16 @@
         f = 3 + n - 3 * d
         before(ROWS * d, f, FACES * d + f)
 
-    speeds = reduce(1)
+    for step in tall_steps:
+        speed_copy(1, 0, tall(step, -1, 1)[1], partner).wait_recv()
+
+    @pl.when(core == 0)
+    def _():
+        speed_copy(1, 0, z, partner).wait_recv()
+
+    speeds = slots[1, 0]
+    for n in range(1, nz):
+        speeds = jnp.maximum(speeds, slots[1, n])
     total = None
     for d in range(3):
         alpha = jnp.max(jnp.where(lane[:1] == d, speeds, 0.0), keepdims=True)
@@ -373,34 +467,29 @@
     halos[0].wait_recv()
     halos[1].wait_recv()
 
-    @pl.loop(0, 6)
+    @pl.loop(0, 3)
     def _(n):
-        cells(n + 8 * (n // 3))
+        cells(n)
+        cells(n + 11)
 
     @pl.loop(0, 6)
     def _(n):
         f = n + 3 * (n // 3)
-        before(0, f, f)
-
-    @pl.loop(0, 6)
-    def _(n):
-        after(0, n + 3 * (n // 3))
+        direct(alphas[0], 0, f, f, uq, cq, fx)
 
     halos[2].wait_recv()
     halos[3].wait_recv()
 
-    @pl.loop(0, 6)
+    @pl.loop(0, 3)
     def _(n):
-        cells(yb + n + 8 * (n // 3))
+        cells(yb + n)
+        cells(yb + n + 11)
 
     @pl.loop(0, 6)
     def _(n):
         f = n + 3 * (n // 3)
-        before(yb, f, FACES + f)
-
-    @pl.loop(0, 6)
-    def _(n):
-        after(1, FACES + n + 3 * (n // 3))
+        direct(alphas[1], yb, f, FACES + f, uq, cq, fx)
+
 
     for k in range(NVAR):
         for r in range(8):
@@ -428,9 +517,17 @@
 
     for copy in halos:
         copy.wait_send()
-    for stage in (0, 1):
-        for n in range(len(steps[stage])):
-            speed_copy(stage, n, me[stage]).wait_send()
+    for copy in first_copies:
+        copy.wait_send()
+
+    @pl.when(core == 0)
+    def _():
+        inward.wait_send()
+
+    @pl.when(core == 1)
+    def _():
+        for copy in second_copies:
+            copy.wait_send()
 
 
 def solution(mesh):
@@ -462,11 +559,11 @@
                 pltpu.VMEM((NVAR, 64, 128), f32),
                 rows(3),
                 pltpu.VMEM((2, 1, 128), f32),
-                pltpu.VMEM((2, 16, 1, 128), f32),
+                pltpu.VMEM((2, 32, 1, 128), f32),
                 pltpu.SemaphoreType.DMA((4,)),
                 pltpu.SemaphoreType.DMA((4,)),
                 pltpu.SemaphoreType.DMA((2, 16)),
-                pltpu.SemaphoreType.DMA((2, 16)),
+                pltpu.SemaphoreType.DMA((2, 32)),
             ],
             compiler_params=pltpu.CompilerParams(
                 collective_id=0, has_side_effects=True, vmem_limit_bytes=36 * 1024 * 1024

time: 31.3 us -> 29.9 us (0.955)
  Pallas kernels: 30.3 us -> 29 us
    pallas_call x1, Pallas kernels: 30.3 us -> 29 us  [shards(): pl.pallas_call(kernel, out_shape=jax.ShapeDtypeStruct((NVAR, 64, 128), f3...]
where the time goes in v5:
time: 29.9 us; the launch traced here: 29.8 us
  Pallas kernels  29 us (97%)
  local copies, waits for them, and re-layouts  0.77 us (3%)
    pallas_call x1, Pallas kernels, shards(): pl.pallas_call(kernel, out_shape=jax.ShapeDtypeStruct((NVAR, 64, 128), f3...  29 us
    unnamed x1, local copies, waits for them, and re-layouts  0.77 us

profile of v5, /device:TPU:1, one launch (start us, length us, event | category | flops | bytes accessed | tf_op | source)
XLA Modules:
  0.0 29.8 jit_solution(17643531739147459976)
XLA Ops:
  0.0 29.0 %shard_map.55 = f32[14,64,128]{2,1,0:T(8,128)S(1)} custom-call(f32[14,64,128]{2,1,0:T(8,128)} %bitcast.4, f32[6,32]{1,0:T(8,128)} %bitcast.5, f32[32]{0:T(128)} %gas_ref.1, s32[9]{0:T(128)} %index_ref.1, s32[1,1,2]{2,1,0:T(1,128)} %kind_ref.1), custom_call_target="tpu_custom_call" | custom-call | tf_op jit(solution)/shard_map/pallas_call | solution.py:542
  29.0 0.8 %copy.7 = f32[14,8,8,128]{3,2,1,0:T(8,128)} copy(f32[14,8,8,128]{3,2,1,0:T(8,128)S(1)} %bitcast.3) | data formatting | bytes 917504

commit v6 on v5

--- a/solution.py
+++ b/solution.py
@@ -47,7 +47,7 @@
         tab_ref[i, 10] = r * a[4] * 0.2
 
 
-def cell_row(u, tab_ref):
+def state_row(u, tab_ref):
     rho = u[0]
     for i in range(1, NS):
         rho = rho + u[i]
@@ -72,6 +72,16 @@
     g = gas / heat
     p = gas * t
     c = jnp.sqrt((1.0 + g) * p * inv)
+    return rho, inv, square, t, g, p, c
+
+
+def speed_row(u, tab_ref):
+    _, inv, _, _, _, _, c = state_row(u, tab_ref)
+    return [jnp.abs(u[k] * inv) + c for k in (NM, T1, T2)]
+
+
+def cell_row(u, tab_ref):
+    rho, inv, square, t, g, p, c = state_row(u, tab_ref)
     half_q = 0.5 * square * inv * inv
     half_g, half_t = 0.5 * g, 0.5 * t
     phi = []
@@ -90,8 +100,7 @@
     flux[NM] = flux[NM] + p
     flux[EN] = (u[EN] + p) * v
     cell += flux
-    speed = [jnp.abs(u[k] * inv) + c for k in (NM, T1, T2)]
-    return cell, speed
+    return cell
 
 
 def correction(d0, d1, d2, d3):
@@ -160,12 +169,15 @@
     return rows + [mean[CZ] * half_acoustic + scalar]
 
 
-def prepare(first, f, i, uq, cq, lf, lu, bf, bu, mean_ref):
-    mean = face_means(first, f, cq)
-    for n in range(NFACE):
-        mean_ref[i, n] = mean[n]
+def prepare(first, f, i, uq, cq, lf, lu, bf, bu, mean_ref, places=(0, 1, 2, 3, 4), linear=True, fresh=True):
+    if fresh:
+        mean = face_means(first, f, cq)
+        for n in range(NFACE):
+            mean_ref[i, n] = mean[n]
+    else:
+        mean = [mean_ref[i, n] for n in range(NFACE)]
     split = splitter(mean)
-    for n in range(5):
+    for n in places:
         here, there = first + f + n, first + f + n + 1
         du = [uq[there, k] - uq[here, k] for k in range(NVAR)]
         df = [cq[there, CF + k] - cq[here, CF + k] for k in range(NVAR)]
@@ -175,6 +187,8 @@
         parts = split(df, du[NM])
         for k in range(NVAR):
             lf[i, n, k] = parts[k]
+    if not linear:
+        return
     for k in range(NVAR):
         f0, f1, f2, f3 = [cq[first + f + n, CF + k] for n in (1, 2, 3, 4)]
         bf[i, k] = 7.0 * (f1 + f2) - (f0 + f3)
@@ -297,47 +311,22 @@
             uq[3 + r, k] = u_ref[ORDER[0][k], 8 * r : 8 * r + 8, :]
 
     def cells(r):
-        cell, speed = cell_row([uq[r, k] for k in range(NVAR)], tab)
+        cell = cell_row([uq[r, k] for k in range(NVAR)], tab)
         for n in range(NCELL):
             cq[r, n] = cell[n]
-        return speed
+
+    def speeds_with(r, best):
+        speed = speed_row([uq[r, k] for k in range(NVAR)], tab)
+        return tuple(jnp.maximum(a, b) for a, b in zip(best, speed))
 
     zero = jnp.zeros((8, 128), jnp.float32)
     best = lax.fori_loop(
-        3, 11, lambda r, best: tuple(jnp.maximum(a, b) for a, b in zip(best, cells(r))), (zero, zero, zero)
+        0, 4, lambda n, best: speeds_with(2 * n + 4, speeds_with(2 * n + 3, best)), (zero, zero, zero)
     )
     row = jnp.zeros((1, 128), jnp.float32)
     for d in range(3):
         row = jnp.where(lane[:1] == d, jnp.max(best[d], keepdims=True), row)
     mine[0] = row
-
-    for pair in range(NVAR // 2):
-        a, b = 2 * pair, 2 * pair + 1
-        turned = jnp.transpose(jnp.concatenate([u_ref[a], u_ref[b]], axis=0))
-        for t in range(8):
-            lo, hi = turned[8 * t : 8 * t + 8], turned[64 + 8 * t : 72 + 8 * t]
-            tmp[a, 8 * t : 8 * t + 8, :] = jnp.where(left, lo, pltpu.roll(hi, 64, 1))
-            tmp[b, 8 * t : 8 * t + 8, :] = jnp.where(left, pltpu.roll(lo, 64, 1), hi)
-    low_wall, high_wall = kind_ref[0, 0, 0] == 1, kind_ref[0, 0, 1] == 1
-    for k in range(NVAR):
-        cz = ORDER[2][k]
-        rows = [tmp[cz, pl.ds(l, 8, stride=8), :] for l in range(8)]
-        for l in range(8):
-            uq[zb + 3 + l, k] = rows[l]
-        sign = -1.0 if k == NM else 1.0
-        for n in range(3):
-            inside = pltpu.roll(rows[7 - n], 1, 0)
-            ghost = jnp.where(low_wall, sign * rows[n], rows[0])
-            edge = jnp.where(left, ghost, pltpu.roll(inside, 64, 1))
-            uq[zb + 2 - n, k] = jnp.where(sub == 0, edge, inside)
-            inside = pltpu.roll(rows[n], 7, 0)
-            ghost = jnp.where(high_wall, sign * rows[7 - n], rows[7])
-            edge = jnp.where(left, pltpu.roll(inside, 64, 1), ghost)
-            uq[zb + 11 + n, k] = jnp.where(sub == 7, edge, inside)
-
-    for k in range(NVAR):
-        for r in range(8):
-            uq[yb + 3 + r, k] = u_ref[ORDER[1][k], pl.ds(r, 8, stride=8), :]
 
     to_core_1 = len(flat_steps) + 2 * len(tall_steps) + 1 + len(beside)
     to_core_0 = len(flat_steps) + 1 + len(beside)
@@ -399,8 +388,48 @@
     ]
     halos[0].start()
 
-    def before(first, f, i):
-        prepare(first, f, i, uq, cq, lf, lu, bf, bu, mean_ref)
+    for pair in range(NVAR // 2):
+        a, b = 2 * pair, 2 * pair + 1
+        turned = jnp.transpose(jnp.concatenate([u_ref[a], u_ref[b]], axis=0))
+        for t in range(8):
+            lo, hi = turned[8 * t : 8 * t + 8], turned[64 + 8 * t : 72 + 8 * t]
+            tmp[a, 8 * t : 8 * t + 8, :] = jnp.where(left, lo, pltpu.roll(hi, 64, 1))
+            tmp[b, 8 * t : 8 * t + 8, :] = jnp.where(left, pltpu.roll(lo, 64, 1), hi)
+    low_wall, high_wall = kind_ref[0, 0, 0] == 1, kind_ref[0, 0, 1] == 1
+    for k in range(NVAR):
+        cz = ORDER[2][k]
+        rows = [tmp[cz, pl.ds(l, 8, stride=8), :] for l in range(8)]
+        for l in range(8):
+            uq[zb + 3 + l, k] = rows[l]
+        sign = -1.0 if k == NM else 1.0
+        for n in range(3):
+            inside = pltpu.roll(rows[7 - n], 1, 0)
+            ghost = jnp.where(low_wall, sign * rows[n], rows[0])
+            edge = jnp.where(left, ghost, pltpu.roll(inside, 64, 1))
+            uq[zb + 2 - n, k] = jnp.where(sub == 0, edge, inside)
+            inside = pltpu.roll(rows[n], 7, 0)
+            ghost = jnp.where(high_wall, sign * rows[7 - n], rows[7])
+            edge = jnp.where(left, pltpu.roll(inside, 64, 1), ghost)
+            uq[zb + 11 + n, k] = jnp.where(sub == 7, edge, inside)
+
+    for k in range(NVAR):
+        for r in range(8):
+            uq[yb + 3 + r, k] = u_ref[ORDER[1][k], pl.ds(r, 8, stride=8), :]
+
+    def before(first, f, i, *how):
+        prepare(first, f, i, uq, cq, lf, lu, bf, bu, mean_ref, *how)
+
+    def rest(d):
+        for f, places, linear in ((1, (0, 1), True), (2, (0,), False), (6, (4,), False), (7, (3, 4), True)):
+            before(ROWS * d, f, FACES * d + f, places, linear, False)
+
+        @pl.loop(0, 2)
+        def _(n):
+            direct(alphas[d], ROWS * d, 8 * n, FACES * d + 8 * n, uq, cq, fx)
+
+        @pl.loop(0, 4)
+        def _(n):
+            after(d, FACES * d + 1 + n + 3 * (n // 2))
 
     @pl.loop(zb, zb + ROWS)
     def _(r):
@@ -431,11 +460,26 @@
     halos[2].start()
     halos[3].start()
 
+    @pl.loop(0, 4)
+    def _(n):
+        cells(2 * n + 3)
+        cells(2 * n + 4)
+
     @pl.loop(0, 6)
     def _(n):
         d = n // 3
         f = 3 + n - 3 * d
         before(ROWS * d, f, FACES * d + f)
+
+    @pl.loop(0, 2)
+    def _(d):
+        for f, places, linear in (
+            (1, (2, 3, 4), False),
+            (2, (1, 2, 3, 4), True),
+            (6, (0, 1, 2, 3), True),
+            (7, (0, 1, 2), False),
+        ):
+            before(ROWS * d, f, FACES * d + f, places, linear)
 
     for step in tall_steps:
         speed_copy(1, 0, tall(step, -1, 1)[1], partner).wait_recv()
@@ -472,10 +516,7 @@
         cells(n)
         cells(n + 11)
 
-    @pl.loop(0, 6)
-    def _(n):
-        f = n + 3 * (n // 3)
-        direct(alphas[0], 0, f, f, uq, cq, fx)
+    rest(0)
 
     halos[2].wait_recv()
     halos[3].wait_recv()
@@ -485,10 +526,7 @@
         cells(yb + n)
         cells(yb + n + 11)
 
-    @pl.loop(0, 6)
-    def _(n):
-        f = n + 3 * (n // 3)
-        direct(alphas[1], yb, f, FACES + f, uq, cq, fx)
+    rest(1)
 
 
     for k in range(NVAR):

time: 29.9 us -> 28.9 us (0.967)
  Pallas kernels: 29 us -> 28 us
    pallas_call x1, Pallas kernels: 29 us -> 28 us  [shards(): pl.pallas_call(kernel, out_shape=jax.ShapeDtypeStruct((NVAR, 64, 128), f3...]
where the time goes in v6:
time: 28.9 us; the launch traced here: 28.8 us
  Pallas kernels  28 us (97%)
  local copies, waits for them, and re-layouts  0.77 us (3%)
    pallas_call x1, Pallas kernels, shards(): pl.pallas_call(kernel, out_shape=jax.ShapeDtypeStruct((NVAR, 64, 128), f3...  28 us
    unnamed x1, local copies, waits for them, and re-layouts  0.77 us

profile of v6, /device:TPU:1, one launch (start us, length us, event | category | flops | bytes accessed | tf_op | source)
XLA Modules:
  0.0 28.8 jit_solution(15881036470202024035)
XLA Ops:
  0.0 28.0 %shard_map.55 = f32[14,64,128]{2,1,0:T(8,128)S(1)} custom-call(f32[14,64,128]{2,1,0:T(8,128)} %bitcast.4, f32[6,32]{1,0:T(8,128)} %bitcast.5, f32[32]{0:T(128)} %gas_ref.1, s32[9]{0:T(128)} %index_ref.1, s32[1,1,2]{2,1,0:T(1,128)} %kind_ref.1), custom_call_target="tpu_custom_call" | custom-call | tf_op jit(solution)/shard_map/pallas_call | solution.py:580
  28.0 0.8 %copy.7 = f32[14,8,8,128]{3,2,1,0:T(8,128)} copy(f32[14,8,8,128]{3,2,1,0:T(8,128)S(1)} %bitcast.3) | data formatting | bytes 917504

commit v7 on v6

--- a/solution.py
+++ b/solution.py
@@ -501,12 +501,15 @@
     def after(d, i):
         finish(alphas[d], i, lf, lu, bf, bu, mean_ref, fx)
 
-    @pl.loop(0, FACES + 6)
-    def _(n):
-        half = n // FACES
-        m = n - FACES * half
-        d = 2 * (1 - half) + half * (m // 3)
-        after(d, FACES * d + (1 - half) * m + half * (3 + m - 3 * (m // 3)))
+    @pl.loop(2 * FACES, 3 * FACES)
+    def _(i):
+        after(2, i)
+
+    @pl.loop(0, 2)
+    def _(d):
+        @pl.loop(3, 6)
+        def _(f):
+            after(d, FACES * d + f)
 
     halos[0].wait_recv()
     halos[1].wait_recv()
@@ -530,15 +533,10 @@
 
 
     for k in range(NVAR):
-        for r in range(8):
-            tmp[ORDER[1][k], 8 * r : 8 * r + 8, :] = fx[FACES + r, k] - fx[FACES + r + 1, k]
-    for k in range(NVAR):
-        for r in range(8):
-            rate = (fx[r, k] - fx[r + 1, k]) + tmp[k, pl.ds(r, 8, stride=8), :]
-            out_ref[k, 8 * r : 8 * r + 8, :] = rate
-    for k in range(NVAR):
-        for r in range(8):
-            tmp[ORDER[2][k], 8 * r : 8 * r + 8, :] = fx[2 * FACES + r, k] - fx[2 * FACES + r + 1, k]
+        for d, turned in ((1, u_ref), (2, tmp)):
+            flux = [fx[d * FACES + r, k] for r in range(FACES)]
+            for r in range(8):
+                turned[ORDER[d][k], 8 * r : 8 * r + 8, :] = flux[r] - flux[r + 1]
     for pair in range(NVAR // 2):
         a, b = 2 * pair, 2 * pair + 1
         low, high = [], []
@@ -548,10 +546,11 @@
             low.append(jnp.where(left, ra, pltpu.roll(rb, 64, 1)))
             high.append(jnp.where(left, pltpu.roll(ra, 64, 1), rb))
         back = jnp.transpose(jnp.concatenate(low + high, axis=0))
-        for r in range(8):
-            here = slice(8 * r, 8 * r + 8)
-            out_ref[a, here] = scale * (out_ref[a, here] + back[8 * r : 8 * r + 8])
-            out_ref[b, here] = scale * (out_ref[b, here] + back[64 + 8 * r : 72 + 8 * r])
+        for k, start in ((a, 0), (b, 64)):
+            flux = [fx[r, k] for r in range(FACES)]
+            for r in range(8):
+                rate = (flux[r] - flux[r + 1]) + u_ref[k, pl.ds(r, 8, stride=8), :]
+                out_ref[k, 8 * r : 8 * r + 8] = scale * (rate + back[start + 8 * r : start + 8 * r + 8])
 
     for copy in halos:
         copy.wait_send()

time: 28.9 us -> 28.7 us (level)
  Pallas kernels: 28 us -> 27.7 us
where the time goes in v7:
time: 28.7 us; the launch traced here: 28.5 us
  Pallas kernels  27.7 us (97%)
  local copies, waits for them, and re-layouts  0.77 us (3%)
    pallas_call x1, Pallas kernels, shards(): pl.pallas_call(kernel, out_shape=jax.ShapeDtypeStruct((NVAR, 64, 128), f3...  27.7 us
    unnamed x1, local copies, waits for them, and re-layouts  0.77 us

profile of v7, /device:TPU:1, one launch (start us, length us, event | category | flops | bytes accessed | tf_op | source)
XLA Modules:
  0.0 28.5 jit_solution(3132728254899676997)
XLA Ops:
  0.0 27.7 %shard_map.55 = f32[14,64,128]{2,1,0:T(8,128)S(1)} custom-call(f32[14,64,128]{2,1,0:T(8,128)} %bitcast.4, f32[6,32]{1,0:T(8,128)} %bitcast.5, f32[32]{0:T(128)} %gas_ref.1, s32[9]{0:T(128)} %index_ref.1, s32[1,1,2]{2,1,0:T(1,128)} %kind_ref.1), custom_call_target="tpu_custom_call" | custom-call | tf_op jit(solution)/shard_map/pallas_call | solution.py:579
  27.7 0.8 %copy.7 = f32[14,8,8,128]{3,2,1,0:T(8,128)} copy(f32[14,8,8,128]{3,2,1,0:T(8,128)S(1)} %bitcast.3) | data formatting | bytes 917504
